TPU v7x, 128 devices: a whole 4x4x4 slice. The times are simulated.
128 devices in a mesh: tok: 32 (over y_lo, z, x), voc: 4 (over y_hi, core).
Axes of the slice: x: 4, y: 4 (y_hi: 2, y_lo: 2; y = y_hi * 2 + y_lo), z: 4, core: 2. Of those that a mesh axis runs over, the one named last changes fastest.
Arguments:
- hidden: bfloat16 [1024, 3584], P('tok'), may hold values from -700 to 700
- teacher_logits: bfloat16 [1024, 81920], P(None, ('tok', 'voc')), may hold values from -300 to 300
- sampled_ids: int32 [1024], P('tok'), may hold values from 0 to 81919
- loss_mask: int32 [1024], P('tok'), may hold values from 0 to 1, as said below
- student_head: bfloat16 [3584, 81920], P(None, ('tok', 'voc')), may hold values from -0.3125 to 0.3125
Outputs:
- loss: float32 [], replicated
- sampled_ratio: float32 [1024], P(('tok', 'voc'))
- hidden_grad: bfloat16 [1024, 3584], P(('tok', 'voc'))
- head_grad: bfloat16 [3584, 81920], P(None, ('tok', 'voc'))
Inputs may be any that keep to these rules, and one draw needn't show every extreme that they name: `loss_mask`: at least one position is valid.
All inputs are finite; a program needn't handle non-finite values.
Results may differ from a plain program's by a relative error of at most 0.02.
Values may be sent and summed in bfloat16 or wider, within the bound.
No kernel may reach another device: no remote copies, remote signals or barrier semaphores. Data moves between devices by JAX's collectives and lax.ppermute only.
A program may use at most 128 MiB of HBM per device.

v0:
```python
import functools
import itertools

import jax
import jax.numpy as jnp
from jax import lax
from jax.experimental import pallas as pl
from jax.experimental.pallas import tpu as pltpu
from jax.sharding import Mesh
from jax.sharding import PartitionSpec as P

TOK = ("tok_0", "tok_1", "tok_2")
TOK_VOC = ("tok_0", "tok_1", "tok_2", "voc_0", "voc_1")
CORE = "voc_1"
DIGIT_BITS = 6
DIGITS = 1 << DIGIT_BITS
EXTRA = 128
INTERPRET = False
XORS = ((1, 3, 2), (3, 1, 2))


def group_of(core, y, z, x):
    return core ^ ((x ^ y ^ z) & 1)


def moved(value, target):
    pairs = []
    for y, z, x, c in itertools.product(range(4), range(4), range(4), range(2)):
        pairs.append(
            tuple(
                ((((v % 2) * 4 + w) * 4 + u) * 2 + v // 2) * 2 + d
                for v, w, u, d in ((y, z, x, c), target(y, z, x, c))
            )
        )
    return lax.ppermute(value, TOK_VOC, pairs)


def swap(value, ring, step):
    def target(y, z, x, c):
        group = group_of(c, y, z, x)
        xor = XORS[group][step]
        at = {"y": y, "z": z, "x": x}
        at[ring] ^= xor
        return at["y"], at["z"], at["x"], group_of(group, at["y"], at["z"], at["x"])

    return moved(value, target)


def to_owner(value, step=None):
    def target(y, z, x, c):
        group = group_of(c, y, z, x)
        return y if step is None else y ^ XORS[group][step], z, x, group

    return moved(value, target)


def swap_core(value):
    return lax.ppermute(value, CORE, [(0, 1), (1, 0)])


def together(*values):
    return lax.optimization_barrier(values)


def token_of_rows(group, z, x, rows):
    n = lax.broadcasted_iota(jnp.int32, (rows, 1), 0)
    quarter = rows // 8
    half, part, top = n // (4 * quarter), (n // (2 * quarter)) % 2, (n // quarter) % 2
    high = half * 2 + top
    low = (n // (quarter // 4)) % 4
    mid = (n // 8) % 2
    first = jnp.where(group == 0, XORS[0][0], XORS[1][0])
    second = jnp.where(group == 0, XORS[0][1], XORS[1][1])

    def place(own, k):
        return own ^ ((k % 2) * first) ^ ((k // 2) * second)

    z_at = jnp.where(part == 0, place(z, high), place(z, low))
    x_at = jnp.where(part == 0, place(x, low), place(x, high))
    return ((((part * 4 + z_at) * 4 + x_at) * 2 + mid) * 2 + group) * 8 + n % 8


def one_hot(rows, columns, dtype):
    return (rows == lax.broadcasted_iota(jnp.int32, (1, columns), 1)).astype(dtype)


VMEM = pl.BlockSpec(memory_space=pltpu.VMEM)
SMEM = pl.BlockSpec(memory_space=pltpu.SMEM)
ANY = pl.BlockSpec(memory_space=pl.ANY)


def near(value):
    return value if INTERPRET else pltpu.with_memory_space_constraint(value, pltpu.VMEM)


def far(value):
    return value if INTERPRET else pltpu.with_memory_space_constraint(value, pltpu.HBM)


def call(kernel, operands, outs, in_specs=None, out_specs=None, flops=10**6, scratch=(), mib=16, aliases={}):
    in_specs = in_specs or [VMEM] * len(operands)
    out_specs = out_specs or [VMEM] * len(outs)
    shapes = [
        pltpu.VMEM(shape, dtype)
        if spec is VMEM and not INTERPRET
        else jax.ShapeDtypeStruct(shape, dtype)
        for (shape, dtype), spec in zip(outs, out_specs)
    ]
    operands = [near(v) if spec is VMEM else v for v, spec in zip(operands, in_specs)]
    return pl.pallas_call(
        kernel,
        out_shape=shapes,
        in_specs=in_specs,
        out_specs=out_specs,
        scratch_shapes=scratch,
        input_output_aliases=aliases,
        compiler_params=pltpu.CompilerParams(vmem_limit_bytes=mib << 20),
        cost_estimate=pl.CostEstimate(flops=flops, bytes_accessed=10**6, transcendentals=0),
        interpret=INTERPRET,
    )(*operands)


def entry_block(group, hidden, ids, mask):
    rows, width = hidden.shape

    def kernel(group_ref, hidden_ref, ids_ref, mask_ref, out_ref, ints, sems):
        starts = [8 * (2 * k + group_ref[0]) for k in range(rows // 16)]
        copies = [
            pltpu.make_async_copy(ids_ref, ints.at[pl.ds(0, 1)], sems.at[0]),
            pltpu.make_async_copy(mask_ref, ints.at[pl.ds(8, 1)], sems.at[1]),
        ]
        for k, at in enumerate(starts):
            copies.append(
                pltpu.make_async_copy(
                    hidden_ref.at[pl.ds(pl.multiple_of(at, 8), 8)],
                    out_ref.at[pl.ds(8 * k, 8), pl.ds(0, width)],
                    sems.at[2 + k],
                )
            )
        for copy in copies:
            copy.start()
        copies[0].wait()
        copies[1].wait()
        lane = lax.broadcasted_iota(jnp.int32, (8, EXTRA), 1)
        for k, at in enumerate(starts):
            row = at + lax.broadcasted_iota(jnp.int32, (8, rows), 0)
            mine = row == lax.broadcasted_iota(jnp.int32, (8, rows), 1)
            one = jnp.sum(jnp.where(mine, ints[0:1], 0), axis=1, keepdims=True)
            extra = jnp.where(
                lane == 0, jnp.sum(jnp.where(mine, ints[8:9], 0), axis=1, keepdims=True), 0
            )
            for d in range(3):
                digit = (one >> (DIGIT_BITS * d)) & (DIGITS - 1)
                extra = jnp.where(lane == d + 1, digit, extra)
            out_ref[8 * k : 8 * k + 8, width:] = extra.astype(jnp.float32).astype(jnp.bfloat16)
        for copy in copies[2:]:
            copy.wait()

    return call(
        kernel,
        (group[None], far(hidden), far(ids[None]), far(mask[None])),
        [((rows // 2, width + EXTRA), jnp.bfloat16)],
        in_specs=[SMEM, ANY, ANY, ANY],
        scratch=[pltpu.VMEM((16, rows), jnp.int32), pltpu.SemaphoreType.DMA((2 + rows // 16,))],
        mib=2,
    )[0]


def joined(*groups, after=()):
    sizes = [len(g) for g in groups]
    pieces = [p for g in groups for p in g]

    def kernel(*refs):
        ins, outs = list(refs[: len(pieces)]), refs[len(refs) - len(groups) :]
        for out_ref, size in zip(outs, sizes):
            at = 0
            for _ in range(size):
                ref = ins.pop(0)
                out_ref[at : at + ref.shape[0]] = ref[...]
                at += ref.shape[0]

    outs = [((sum(p.shape[0] for p in g), g[0].shape[1]), g[0].dtype) for g in groups]
    return call(kernel, [*pieces, *after], outs, mib=4)


def turned(a, b, width):
    rows = a.shape[0]
    cuts = 7

    def kernel(a_ref, b_ref, out_ref):
        for k in range(cuts):
            at = slice(k * width // cuts, (k + 1) * width // cuts)
            out_ref[at, :rows] = a_ref[:, at].T
            out_ref[at, rows:] = b_ref[:, at].T

    return call(kernel, [a, b], [((width, 2 * rows), a.dtype)], flops=10**9)[0]


def added(groups, blocks):
    sizes = [len(g) for g in groups]
    parts = [p for g in groups for p in g]

    def kernel(*refs):
        ins, outs = list(refs[: len(parts)]), list(refs[len(parts) :])
        for size in sizes:
            terms = [ins.pop(0) for _ in range(size)]
            cut = terms[0].shape[0] // blocks
            for k in range(blocks):
                at = slice(k * cut, (k + 1) * cut)
                total = sum(t[at].astype(jnp.float32) for t in terms[1:])
                outs.pop(0)[...] = (total + terms[0][at].astype(jnp.float32)).astype(jnp.bfloat16)

    outs = [
        ((g[0].shape[0] // blocks, g[0].shape[1]), jnp.bfloat16) for g in groups for _ in range(blocks)
    ]
    return call(kernel, parts, outs, mib=4)


def added_by_place(groups, spot):
    sizes = [len(g) for g in groups]
    parts = [p for g in groups for p in g]
    rows, width = parts[0].shape

    def kernel(spot_ref, *refs):
        ins, outs, sums = list(refs[: len(parts)]), refs[len(parts) : -1], refs[-1]
        for k, size in enumerate(sizes):
            terms = [ins.pop(0) for _ in range(size)]
            sums[k * rows : (k + 1) * rows] = sum(t[...].astype(jnp.float32) for t in terms)
        for k, out_ref in enumerate(outs):
            step = 0 if k == 0 else jnp.where(spot_ref[0] == 0, XORS[0][k - 1], XORS[1][k - 1])
            y = (spot_ref[2] * 2 + spot_ref[1]) ^ step
            at = pl.multiple_of(((y & 1) * 2 + (y >> 1)) * 8, 8)
            out_ref[...] = sums[pl.ds(at, 8), :].astype(jnp.bfloat16)

    blocks = len(groups) * rows // 8
    return call(
        kernel,
        [spot, *parts],
        [((8, width), jnp.bfloat16)] * blocks,
        in_specs=[SMEM] + [VMEM] * len(parts),
        scratch=[pltpu.VMEM((len(groups) * rows, width), jnp.float32)],
        mib=4,
    )


def combined(parts, spot=None):
    shape = parts[0].shape
    n = len(parts)

    def kernel(*refs):
        ins, outs = refs[:n], refs[n:]
        smax = functools.reduce(jnp.maximum, [r[0:1] for r in ins])
        tmax = functools.reduce(jnp.maximum, [r[3:4] for r in ins])
        stot = cross = ttot = pick = 0.0
        for r in ins:
            factor = jnp.exp(r[0:1] - smax)
            stot, cross = stot + r[1:2] * factor, cross + r[2:3] * factor
            ttot = ttot + r[4:5] * jnp.exp(r[3:4] - tmax)
            pick = pick + r[5:6]
        mask = ins[0][6:7]
        rows = [smax, stot, cross, tmax, ttot, pick, mask, mask]
        if spot is not None:
            spot_ref, *outs = outs
            student_shift, teacher_shift = smax + jnp.log(stot), tmax + jnp.log(ttot)
            apart = student_shift - teacher_shift
            row_kl = cross / stot - apart
            rows = [student_shift, apart + row_kl] + [mask] * 6
            lane = lax.broadcasted_iota(jnp.int32, (8, 128), 1)
            total = jnp.sum(mask * row_kl, axis=1, keepdims=True)
            count = jnp.sum(mask, axis=1, keepdims=True)
            row = (spot_ref[3] >> 1) * 8 + lax.broadcasted_iota(jnp.int32, (8, shape[1]), 0)
            mine = row == lax.broadcasted_iota(jnp.int32, (8, shape[1]), 1)
            ratio = jnp.sum(jnp.where(mine, pick - apart, 0.0), axis=1, keepdims=True)
            here = lane == lax.broadcasted_iota(jnp.int32, (8, 128), 0)
            ratio = jnp.sum(jnp.where(here, ratio, 0.0), axis=0, keepdims=True)
            line = lax.broadcasted_iota(jnp.int32, (8, 128), 0)
            outs[1][...] = jnp.where(line == 0, total, jnp.where(line == 1, count, ratio))
        for k, row in enumerate(rows):
            outs[0][k : k + 1] = row

    out = (shape, jnp.float32)
    if spot is None:
        return call(kernel, parts, [out], mib=2)[0]
    outs = [out, ((8, 128), jnp.float32)]
    return call(kernel, [*parts, spot], outs, in_specs=[VMEM] * n + [SMEM], mib=2)


def side_by_side(head, head_in):
    width, columns = head.shape
    cuts = 4

    def kernel(h_ref, g_ref, out_ref, mark_ref, sems):
        mark_ref[...] = jnp.zeros(mark_ref.shape, jnp.float32)
        copies = []
        for k in range(cuts):
            at = pl.ds(k * width // cuts, width // cuts)
            for ref, column in ((h_ref, 0), (g_ref, columns)):
                copies.append(
                    pltpu.make_async_copy(
                        ref.at[at], out_ref.at[at, pl.ds(column, columns)], sems.at[len(copies)]
                    )
                )
        for copy in copies:
            copy.start()
        for copy in copies:
            copy.wait()

    return call(
        kernel,
        (far(head), far(head_in)),
        [((width, 2 * columns), head.dtype), ((8, 128), jnp.float32)],
        in_specs=[ANY, ANY],
        scratch=[pltpu.SemaphoreType.DMA((2 * cuts,))],
        flops=4 * 10**9,
        mib=2,
    )


def logits_and_stats(spot, a, b, heads, teacher, teacher_in, places, which, before=None):
    f32 = jnp.float32
    width, both = heads.shape
    columns = both // 2
    part, rows, tokens = a.shape[0], 2 * a.shape[0], places.shape[0]
    chunk = 32

    def kernel(spot_ref, a_ref, b_ref, h_ref, t_ref, u_ref, p_ref, *rest):
        out_ref, stats_ref, states, placed = rest[-4:]
        states[:part] = a_ref[:, :width]
        states[part:] = b_ref[:, :width]
        out_ref[...] = jnp.dot(states[...], h_ref[...], preferred_element_type=f32)
        lanes = lax.broadcasted_iota(jnp.int32, (1, both), 1)
        base, other_base = spot_ref[3] * columns, (spot_ref[3] ^ 1) * columns
        column = jnp.where(lanes < columns, base + lanes, other_base + lanes - columns)
        spots = lax.broadcasted_iota(jnp.int32, (1, tokens), 1)
        placed[...] = jnp.zeros(placed.shape, f32)
        for k in range(rows // chunk):
            ref, at = (a_ref, k * chunk) if k * chunk < part else (b_ref, k * chunk - part)
            here = slice(k * chunk, (k + 1) * chunk)
            there = slice(which * rows + k * chunk, which * rows + (k + 1) * chunk)
            student, note = out_ref[here, :], ref[at : at + chunk, width:].astype(f32)
            teacher = jnp.concatenate([t_ref[there, :], u_ref[there, :]], axis=1).astype(f32)
            ids = note[:, 1:2] + DIGITS * note[:, 2:3] + DIGITS**2 * note[:, 3:4]
            chosen = ids.astype(jnp.int32) == column
            smax = jnp.max(student, axis=1, keepdims=True)
            tmax = jnp.max(teacher, axis=1, keepdims=True)
            shifted = jnp.exp(student - smax)
            differ = student - teacher
            sums = [
                smax,
                jnp.sum(shifted, axis=1, keepdims=True),
                jnp.sum(shifted * differ, axis=1, keepdims=True),
                tmax,
                jnp.sum(jnp.exp(teacher - tmax), axis=1, keepdims=True),
                jnp.sum(jnp.where(chosen, differ, 0.0), axis=1, keepdims=True),
                note[:, :1],
            ]
            mine = p_ref[there, :] == spots
            for r, value in enumerate(sums):
                found = jnp.where(mine, value, 0.0).reshape(chunk // 8, 8, tokens)
                placed[r] += jnp.sum(found, axis=0)
        for r in range(8):
            row = jnp.sum(placed[r], axis=0, keepdims=True)
            stats_ref[r : r + 1] = row if before is None else row + rest[0][r : r + 1]

    operands = [spot, a, b, heads, teacher, teacher_in, places]
    if before is not None:
        operands.append(before)
    return call(
        kernel,
        operands,
        [((rows, both), f32), ((8, tokens), f32)],
        in_specs=[SMEM] + [VMEM] * (len(operands) - 1),
        scratch=[pltpu.VMEM((rows, width), jnp.bfloat16), pltpu.VMEM((8, 8, tokens), f32)],
        flops=2 * rows * width * both,
    )


def gradients(student, shifts, heads, teacher, teacher_in, places, which):
    f32, bf16 = jnp.float32, jnp.bfloat16
    width, both = heads.shape
    columns = both // 2
    rows, tokens = student.shape[0], places.shape[0]
    part = rows // 2
    chunk, cuts = 32, 7

    def kernel(s_ref, c_ref, h_ref, t_ref, u_ref, p_ref, a_ref, b_ref, d_ref, e_ref, all_d):
        spots = lax.broadcasted_iota(jnp.int32, (1, tokens), 1)
        for k in range(rows // chunk):
            here = slice(k * chunk, (k + 1) * chunk)
            there = slice(which * rows + k * chunk, which * rows + (k + 1) * chunk)
            mine = p_ref[there, :] == spots

            def of_row(r):
                return jnp.sum(jnp.where(mine, c_ref[r : r + 1], 0.0), axis=1, keepdims=True)

            student = s_ref[here, :]
            teacher = jnp.concatenate([t_ref[there, :], u_ref[there, :]], axis=1).astype(f32)
            probs = of_row(2) * jnp.exp(student - of_row(0))
            found = (probs * (student - teacher - of_row(1))).astype(bf16)
            all_d[here, :] = found
            d_ref[here, :] = found[:, :columns]
            e_ref[here, :] = found[:, columns:]
        for k in range(cuts):
            at = slice(k * width // cuts, (k + 1) * width // cuts)
            product = lax.dot_general(
                all_d[...], h_ref[at, :], (((1,), (1,)), ((), ())), preferred_element_type=f32
            ).astype(bf16)
            a_ref[:, at] = product[:part]
            b_ref[:, at] = product[part:]

    return call(
        kernel,
        [student, shifts, heads, teacher, teacher_in, places],
        [((part, width), bf16)] * 2 + [((rows, columns), bf16)] * 2,
        scratch=[pltpu.VMEM((rows, both), bf16)],
        flops=2 * rows * width * both,
    )


def head_gradient(states, dlogits, blocks, before=None):
    bf16 = jnp.bfloat16
    width, columns = states[0].shape[0], dlogits[0].shape[1]
    block = 512
    tokens = sum(d.shape[0] for d in dlogits)
    n, m = len(states), len(states) + len(dlogits)

    def kernel(*refs):
        pieces, others = refs[:n], refs[n:m]
        out_ref, right, found, sems = refs[-4:]
        at = 0
        for ref in others:
            right[at : at + ref.shape[0]] = ref[...]
            at += ref.shape[0]
        copies = []
        for j, k in enumerate(blocks):
            left = jnp.concatenate([r[k * block : (k + 1) * block, :] for r in pieces], axis=1)
            product = jnp.dot(left, right[...], preferred_element_type=jnp.float32).astype(bf16)
            slot = j % 2
            if j >= 2:
                copies[j - 2].wait()
            found[slot] = product
            copies.append(
                pltpu.make_async_copy(
                    found.at[slot], out_ref.at[pl.ds(k * block, block)], sems.at[slot]
                )
            )
            copies[j].start()
        copies[-2].wait()
        copies[-1].wait()

    operands, specs = [*states, *dlogits], [VMEM] * m
    if before is not None:
        operands, specs = [*operands, before], [*specs, ANY]
    return call(
        kernel,
        operands,
        [((width, columns), bf16)],
        in_specs=specs,
        out_specs=[ANY],
        scratch=[
            pltpu.VMEM((tokens, columns), bf16),
            pltpu.VMEM((2, block, columns), bf16),
            pltpu.SemaphoreType.DMA((2,)),
        ],
        flops=2 * tokens * len(blocks) * block * columns,
        aliases={} if before is None else {m: 0},
    )[0]


def per_device(hidden, teacher_logits, sampled_ids, loss_mask, student_head):
    f32, bf16 = jnp.float32, jnp.bfloat16
    core, y_low = lax.axis_index(CORE), lax.axis_index("tok_0")
    z, x = lax.axis_index("tok_1"), lax.axis_index("tok_2")
    position = lax.axis_index(TOK_VOC)
    group = group_of(core, y_low, z, x)
    width, _ = student_head.shape
    tokens = teacher_logits.shape[0]
    rows = tokens // 2

    block = entry_block(group, hidden, sampled_ids, loss_mask)
    token = token_of_rows(group, z, x, rows)
    token_other = token_of_rows(1 - group, z, x, rows)
    places = (token // 16) * 8 + token % 8
    spot = jnp.stack([group, y_low, lax.axis_index("voc_0"), position])
    other = swap(block, "y", 0)
    head_in = swap_core(student_head)
    teacher_send = jnp.dot(one_hot(token_other, tokens, bf16), teacher_logits)
    own_group = jnp.broadcast_to(group == core, (8,))
    other, teacher_send, spot, places, own_group = together(
        other, teacher_send, spot, places, own_group
    )
    teacher_in = swap_core(teacher_send)
    near_a = jnp.where(y_low == 0, block, other)
    near_b = jnp.where(y_low == 0, other, block)

    pieces_a, pieces_b = [near_a], [near_b]
    for step in range(3):
        pieces_a.append(swap(near_a, "x", step))
        pieces_b.append(swap(near_b, "z", step))
    teacher = jnp.dot(one_hot(token, tokens, bf16), teacher_logits)
    *pieces, teacher = together(*pieces_a, *pieces_b, teacher)
    near_a, near_b = joined(pieces[:4], pieces[4:])

    far_a, far_b = swap(near_a, "z", 0), swap(near_b, "x", 0)
    heads, mark = side_by_side(student_head, head_in)
    near_a, near_b = joined((near_a, far_a), (near_b, far_b), after=(mark,))

    far_a, far_b = swap(near_a, "z", 1), swap(near_b, "x", 1)
    shared = (heads, teacher, teacher_in, places)
    near_other = swap_core(near_a), swap_core(near_b)
    student_near, stats = logits_and_stats(spot, near_a, near_b, *shared, 0)
    states = [turned(near_a, near_b, width)]
    far_a, far_b, student_near, stats, states[0] = together(
        far_a, far_b, student_near, stats, states[0]
    )
    student_far, stats = logits_and_stats(spot, far_a, far_b, *shared, 1, stats)
    pair = (far_a, far_b)
    for ring in ("x", "z", "y"):
        parts = [stats]
        for step in range(3):
            parts.append(swap(stats, ring, step))
        state = turned(*pair, width)
        states.append(state)
        if ring == "z":
            far_a, far_b, parts[0] = together(far_a, far_b, parts[0])
            pair = swap_core(far_a), swap_core(far_b)
        *parts, states[-1] = together(*parts, state)
        stats = combined(parts, spot if ring == "y" else None)
        if ring == "x":
            *pair, stats = together(*near_other, stats)
    stats, sums = stats

    far_sum_a, far_sum_b, *far_d = gradients(student_far, stats, *shared, 1)
    far_sum_a, far_sum_b, stats_later = together(far_sum_a, far_sum_b, stats)
    a_in, b_in = swap(far_sum_a, "z", 1), swap(far_sum_b, "x", 1)
    far_d_in = swap_core(far_d[1])
    near_sum_a, near_sum_b, *near_d = gradients(student_near, stats_later, *shared, 0)
    near_d_in = swap_core(near_d[1])
    all_d = (near_d[0], far_d[0], near_d_in, far_d_in)
    head_grad = head_gradient(states, all_d, range(4))
    a_in, b_in, near_sum_a, near_sum_b, head_grad, other_sums = together(
        a_in, b_in, near_sum_a, near_sum_b, head_grad, swap_core(sums)
    )
    keep_a, send_a, keep_b, send_b = added(((near_sum_a, a_in), (near_sum_b, b_in)), 2)
    a_in, b_in = swap(send_a, "z", 0), swap(send_b, "x", 0)
    head_grad = head_gradient(states, all_d, range(4, width // 512), head_grad)
    a_in, b_in, head_grad = together(a_in, b_in, head_grad)
    keep_a, *send_a, keep_b, to_1, to_2, to_3 = added(((keep_a, a_in), (keep_b, b_in)), 4)
    arrived = [
        swap(part, ring, step)
        for step in range(3)
        for part, ring in ((send_a[step], "x"), ((to_1, to_2, to_3)[step], "z"))
    ]
    loss = (sums[0, 0] + other_sums[0, 0]) / (sums[1, 0] + other_sums[1, 0])
    sampled_ratio = jnp.where(own_group, sums[2, :8], other_sums[2, :8])
    *arrived, loss, sampled_ratio = together(*arrived, loss, sampled_ratio)
    keep, *send = added_by_place(((keep_a, *arrived[0::2]), (keep_b, *arrived[1::2])), spot)
    arrived = [to_owner(part, step) for step, part in enumerate(send)]
    parts = [to_owner(keep), *arrived]
    hidden_grad = sum(p.astype(f32) for p in parts).astype(bf16)
    return (loss, sampled_ratio, hidden_grad, head_grad)


def solution(mesh):
    split = Mesh(mesh.devices.reshape(2, 4, 4, 2, 2), TOK_VOC)
    in_specs = (P(TOK, None), P(None, TOK_VOC), P(TOK), P(TOK), P(None, TOK_VOC))
    out_specs = (P(), P(TOK_VOC), P(TOK_VOC, None), P(None, TOK_VOC))

    return jax.shard_map(
        per_device, mesh=split, in_specs=in_specs, out_specs=out_specs, check_vma=False
    )
```

profile of v0, /device:TPU:1, one launch (start us, length us, event | category | flops | bytes accessed | tf_op | source)
XLA Modules:
  0.0 133.6 jit_solution(12721062233845469154)
XLA Ops:
  3.0 2.9 %collective-permute-start = (bf16[16,3712]{1,0:T(8,128)(2,1)S(1)}, bf16[16,3712]{1,0:T(8,128)(2,1)S(1)}, u32[]{:S(2)}, u32[]{:S(2)}) collective-permute-start(bf16[16,3712]{1,0:T(8,128)(2,1)S(1)} %shard_map.84), channel_id=1, source_target_pairs={{0,65},{1,66},{4,71},{5,68},{8,73},{9,74},{12,79},{13,76},{16,83},... | collective-permute-start | bytes 356360 | tf_op jit(solution)/shard_map/ppermute | solution.py:35
  8.6 2.7 %collective-permute-start.1 = (bf16[16,3712]{1,0:T(8,128)(2,1)S(1)}, bf16[16,3712]{1,0:T(8,128)(2,1)S(1)}, u32[]{:S(2)}, u32[]{:S(2)}) collective-permute-start(bf16[16,3712]{1,0:T(8,128)(2,1)S(1)} %get-tuple-element.102.refs_0_), channel_id=1, source_target_pairs={{0,5},{1,12},{4,9},{5,0},{8,13},{9,4},{12,1},{13,8},{16,29},{17,20... | collective-permute-start | bytes 356360 | tf_op jit(solution)/shard_map/ppermute | solution.py:35
  12.9 4.2 %collective-permute-start.4 = (bf16[16,3712]{1,0:T(8,128)(2,1)S(1)}, bf16[16,3712]{1,0:T(8,128)(2,1)S(1)}, u32[]{:S(2)}, u32[]{:S(2)}) collective-permute-start(bf16[16,3712]{1,0:T(8,128)(2,1)S(1)} %get-tuple-element.106.refs_4_), channel_id=1, source_target_pairs={{0,17},{1,48},{4,53},{5,20},{8,25},{9,56},{12,61},{13,28},{16,33},... | collective-permute-start | bytes 356360 | tf_op jit(solution)/shard_map/ppermute | solution.py:35
  17.2 3.2 %collective-permute-start.6 = (bf16[16,3712]{1,0:T(8,128)(2,1)S(1)}, bf16[16,3712]{1,0:T(8,128)(2,1)S(1)}, u32[]{:S(2)}, u32[]{:S(2)}) collective-permute-start(bf16[16,3712]{1,0:T(8,128)(2,1)S(1)} %get-tuple-element.106.refs_4_), channel_id=1, source_target_pairs={{0,32},{1,33},{4,36},{5,37},{8,40},{9,41},{12,44},{13,45},{16,48},... | collective-permute-start | bytes 356360 | tf_op jit(solution)/shard_map/ppermute | solution.py:35
  24.9 2.4 %collective-permute-start.7 = (bf16[64,3712]{1,0:T(8,128)(2,1)S(1)}, bf16[64,3712]{1,0:T(8,128)(2,1)S(1)}, u32[]{:S(2)}, u32[]{:S(2)}) collective-permute-start(bf16[64,3712]{1,0:T(8,128)(2,1)S(1)} %get-tuple-element.110.refs_0_), channel_id=1, source_target_pairs={{0,17},{1,48},{4,53},{5,20},{8,25},{9,56},{12,61},{13,28},{16,33},... | collective-permute-start | bytes 1425416 | tf_op jit(solution)/shard_map/ppermute | solution.py:35
  27.3 2.7 %collective-permute-start.8 = (bf16[64,3712]{1,0:T(8,128)(2,1)S(1)}, bf16[64,3712]{1,0:T(8,128)(2,1)S(1)}, u32[]{:S(2)}, u32[]{:S(2)}) collective-permute-start(bf16[64,3712]{1,0:T(8,128)(2,1)S(1)} %get-tuple-element.111.refs_2_), channel_id=1, source_target_pairs={{0,5},{1,12},{4,9},{5,0},{8,13},{9,4},{12,1},{13,8},{16,29},{17,20... | collective-permute-start | bytes 1425416 | tf_op jit(solution)/shard_map/ppermute | solution.py:35
  30.0 3.7 %shard_map.86 = (bf16[3584,1280]{1,0:T(8,128)(2,1)S(1)}, f32[8,128]{1,0:T(8,128)S(1)}) custom-call(bf16[3584,640]{1,0:T(8,128)(2,1)} %h_ref.1, bf16[3584,640]{1,0:T(8,128)(2,1)} %collective-permute-done.9.g_ref), custom_call_target="tpu_custom_call" | custom-call | flops 4000000000 | bytes 1000000 | tf_op jit(solution)/shard_map/pallas_call | solution.py:110
  34.3 2.3 %collective-permute-done.8.refs_3_ = bf16[64,3712]{1,0:T(8,128)(2,1)S(1)} collective-permute-done((bf16[64,3712]{1,0:T(8,128)(2,1)S(1)}, bf16[64,3712]{1,0:T(8,128)(2,1)S(1)}, u32[]{:S(2)}, u32[]{:S(2)}) %collective-permute-start.8) | collective-permute-done | bytes 475168 | tf_op jit(solution)/shard_map/ppermute | solution.py:35
  39.4 3.9 %shard_map.88 = (f32[256,1280]{1,0:T(8,128)S(1)}, f32[8,512]{1,0:T(8,128)S(1)}) custom-call(s32[4]{0:T(128)S(1)} %pad_add_fusion.spot_ref.refs_4_, bf16[128,3712]{1,0:T(8,128)(2,1)S(1)} %get-tuple-element.113.a_ref, bf16[128,3712]{1,0:T(8,128)(2,1)S(1)} %get-tuple-element.114.b_ref, bf16[3584,1280]{1,0:T(8,128)(2,1)S(1)} %get-tuple-element.115.h_ref, ...), custom_call_target="tpu_custom_call" | custom-call | flops 2348810240 | bytes 1000000 | tf_op jit(solution)/shard_map/pallas_call | solution.py:110
  43.3 7.1 %collective-permute-done.10.a_ref = bf16[128,3712]{1,0:T(8,128)(2,1)S(1)} collective-permute-done((bf16[128,3712]{1,0:T(8,128)(2,1)S(1)}, bf16[128,3712]{1,0:T(8,128)(2,1)S(1)}, u32[]{:S(2)}, u32[]{:S(2)}) %collective-permute-start.10) | collective-permute-done | bytes 950304 | tf_op jit(solution)/shard_map/ppermute | solution.py:35
  50.7 3.8 %shard_map.90 = (f32[256,1280]{1,0:T(8,128)S(1)}, f32[8,512]{1,0:T(8,128)S(1)}) custom-call(s32[4]{0:T(128)S(1)} %pad_add_fusion.spot_ref.refs_4_, bf16[128,3712]{1,0:T(8,128)(2,1)S(1)} %collective-permute-done.10.a_ref, bf16[128,3712]{1,0:T(8,128)(2,1)S(1)} %collective-permute-done.11.b_ref, bf16[3584,1280]{1,0:T(8,128)(2,1)S(1)} %get-tuple-element.115.h_ref, ...), custom_call_target="tpu_custom_call" | custom-call | flops 2348810240 | bytes 1000000 | tf_op jit(solution)/shard_map/pallas_call | solution.py:110
  54.5 2.7 %collective-permute-start.15 = (f32[8,512]{1,0:T(8,128)S(1)}, f32[8,512]{1,0:T(8,128)S(1)}, u32[]{:S(2)}, u32[]{:S(2)}) collective-permute-start(f32[8,512]{1,0:T(8,128)S(1)} %get-tuple-element.126.refs_0_), channel_id=1, source_target_pairs={{0,5},{1,12},{4,9},{5,0},{8,13},{9,4},{12,1},{13,8},{16,29},{17,20... | collective-permute-start | bytes 49160 | tf_op jit(solution)/shard_map/ppermute | solution.py:35
  62.0 2.1 %collective-permute-start.18 = (f32[8,512]{1,0:T(8,128)S(1)}, f32[8,512]{1,0:T(8,128)S(1)}, u32[]{:S(2)}, u32[]{:S(2)}) collective-permute-start(f32[8,512]{1,0:T(8,128)S(1)} %shard_map.92.refs_0_), channel_id=1, source_target_pairs={{0,17},{1,48},{4,53},{5,20},{8,25},{9,56},{12,61},{13,28},{16,33},... | collective-permute-start | bytes 49160 | tf_op jit(solution)/shard_map/ppermute | solution.py:35
  68.3 5.7 %collective-permute-start.21 = (f32[8,512]{1,0:T(8,128)S(1)}, f32[8,512]{1,0:T(8,128)S(1)}, u32[]{:S(2)}, u32[]{:S(2)}) collective-permute-start(f32[8,512]{1,0:T(8,128)S(1)} %shard_map.94.refs_0_), channel_id=1, source_target_pairs={{0,65},{1,66},{4,71},{5,68},{8,73},{9,74},{12,79},{13,76},{16,83},... | collective-permute-start | bytes 49160 | tf_op jit(solution)/shard_map/ppermute | solution.py:35
  78.7 3.1 %shard_map.97 = (bf16[128,3584]{1,0:T(8,128)(2,1)S(1)}, bf16[128,3584]{1,0:T(8,128)(2,1)S(1)}, bf16[256,640]{1,0:T(8,128)(2,1)S(1)}, bf16[256,640]{1,0:T(8,128)(2,1)S(1)}) custom-call(f32[256,1280]{1,0:T(8,128)S(1)} %get-tuple-element.124.s_ref, f32[8,512]{1,0:T(8,128)S(1)} %get-tuple-element.150.c_ref, bf16[3584,1280]{1,0:T(8,128)(2,1)S(1)} %get-tuple-element.115.h_ref, ...), custom_call_target="tpu_custom_call" | custom-call | flops 2348810240 | bytes 1000000 | tf_op jit(solution)/shard_map/pallas_call | solution.py:110
  81.8 2.1 %collective-permute-start.26 = (bf16[128,3584]{1,0:T(8,128)(2,1)S(1)}, bf16[128,3584]{1,0:T(8,128)(2,1)S(1)}, u32[]{:S(2)}, u32[]{:S(2)}) collective-permute-start(bf16[128,3584]{1,0:T(8,128)(2,1)S(1)} %get-tuple-element.147), channel_id=1, source_target_pairs={{0,49},{1,16},{4,21},{5,52},{8,57},{9,24},{12,29},{13,60},{16,1},{... | collective-permute-start | bytes 2752520 | tf_op jit(solution)/shard_map/ppermute | solution.py:35
  84.8 3.1 %shard_map.98 = (bf16[128,3584]{1,0:T(8,128)(2,1)S(1)}, bf16[128,3584]{1,0:T(8,128)(2,1)S(1)}, bf16[256,640]{1,0:T(8,128)(2,1)S(1)}, bf16[256,640]{1,0:T(8,128)(2,1)S(1)}) custom-call(f32[256,1280]{1,0:T(8,128)S(1)} %get-tuple-element.149.s_ref, f32[8,512]{1,0:T(8,128)S(1)} %get-tuple-element.150.c_ref, bf16[3584,1280]{1,0:T(8,128)(2,1)S(1)} %get-tuple-element.115.h_ref, ...), custom_call_target="tpu_custom_call" | custom-call | flops 2348810240 | bytes 1000000 | tf_op jit(solution)/shard_map/pallas_call | solution.py:110
  90.7 5.2 %shard_map.99.refs_8_ = bf16[3584,640]{1,0:T(8,128)(2,1)} custom-call(bf16[3584,256]{1,0:T(8,128)(2,1)S(1)} %shard_map.89.refs_0_, bf16[3584,256]{1,0:T(8,128)(2,1)S(1)} %shard_map.91.refs_1_, bf16[3584,256]{1,0:T(8,128)(2,1)S(1)} %shard_map.93.refs_2_, bf16[3584,256]{1,0:T(8,128)(2,1)S(1)} %shard_map.95.refs_3_, ...), custom_call_target="tpu_custom_call" | custom-call | flops 2684354560 | bytes 1000000 | tf_op jit(solution)/shard_map/pallas_call | solution.py:110
  100.2 3.6 %shard_map.101 = bf16[3584,640]{1,0:T(8,128)(2,1)} custom-call(bf16[3584,256]{1,0:T(8,128)(2,1)S(1)} %shard_map.89.refs_0_, bf16[3584,256]{1,0:T(8,128)(2,1)S(1)} %shard_map.91.refs_1_, bf16[3584,256]{1,0:T(8,128)(2,1)S(1)} %shard_map.93.refs_2_, bf16[3584,256]{1,0:T(8,128)(2,1)S(1)} %shard_map.95.refs_3_, ...), custom_call_target="tpu_custom_call", output_to_operand_aliasing={{}: (8, {})} | custom-call | flops 2013265920 | bytes 1000000 | tf_op jit(solution)/shard_map/pallas_call | solution.py:110
  103.7 2.9 %collective-permute-done.31.refs_1_ = bf16[64,3584]{1,0:T(8,128)(2,1)S(1)} collective-permute-done((bf16[64,3584]{1,0:T(8,128)(2,1)S(1)}, bf16[64,3584]{1,0:T(8,128)(2,1)S(1)}, u32[]{:S(2)}, u32[]{:S(2)}) %collective-permute-start.31) | collective-permute-done | bytes 458784 | tf_op jit(solution)/shard_map/ppermute | solution.py:35
  114.0 3.8 %collective-permute-start.37 = (bf16[16,3584]{1,0:T(8,128)(2,1)S(1)}, bf16[16,3584]{1,0:T(8,128)(2,1)S(1)}, u32[]{:S(2)}, u32[]{:S(2)}) collective-permute-start(bf16[16,3584]{1,0:T(8,128)(2,1)S(1)} %get-tuple-element.177), channel_id=1, source_target_pairs={{0,8},{1,9},{4,12},{5,13},{8,0},{9,1},{12,4},{13,5},{16,24},{17,25... | collective-permute-start | bytes 344072 | tf_op jit(solution)/shard_map/ppermute | solution.py:35
  117.8 2.4 %collective-permute-start.38 = (bf16[16,3584]{1,0:T(8,128)(2,1)S(1)}, bf16[16,3584]{1,0:T(8,128)(2,1)S(1)}, u32[]{:S(2)}, u32[]{:S(2)}) collective-permute-start(bf16[16,3584]{1,0:T(8,128)(2,1)S(1)} %get-tuple-element.178), channel_id=1, source_target_pairs={{0,32},{1,33},{4,36},{5,37},{8,40},{9,41},{12,44},{13,45},{16,48},... | collective-permute-start | bytes 344072 | tf_op jit(solution)/shard_map/ppermute | solution.py:35
  126.3 2.6 %collective-permute-start.40 = (bf16[8,3584]{1,0:T(8,128)(2,1)S(1)}, bf16[8,3584]{1,0:T(8,128)(2,1)S(1)}, u32[]{:S(2)}, u32[]{:S(2)}) collective-permute-start(bf16[8,3584]{1,0:T(8,128)(2,1)S(1)} %get-tuple-element.192), channel_id=1, source_target_pairs={{0,64},{1,67},{4,71},{5,68},{8,72},{9,75},{12,79},{13,76},{16,83},... | collective-permute-start | bytes 172040 | tf_op jit(solution)/shard_map/ppermute | solution.py:35
  129.7 2.2 %collective-permute-done.40 = bf16[8,3584]{1,0:T(8,128)(2,1)S(1)} collective-permute-done((bf16[8,3584]{1,0:T(8,128)(2,1)S(1)}, bf16[8,3584]{1,0:T(8,128)(2,1)S(1)}, u32[]{:S(2)}, u32[]{:S(2)}) %collective-permute-start.40) | collective-permute-done | bytes 57376 | tf_op jit(solution)/shard_map/ppermute | solution.py:35
  (96 shorter events, 48.5 us)
Async XLA Ops:
  0.6 29.4 %collective-permute-start.9 = (bf16[3584,640]{1,0:T(8,128)(2,1)}, bf16[3584,640]{1,0:T(8,128)(2,1)}, u32[]{:S(2)}, u32[]{:S(2)}) collective-permute-start(bf16[3584,640]{1,0:T(8,128)(2,1)} %h_ref.1), channel_id=1, source_target_pairs={{0,1},{1,0},{2,3},{3,2},{4,5},{5,4},{6,7},{7,6},{8,9},{9,8},{10,11... | collective-permute-start | bytes 13762568 | tf_op jit(solution)/shard_map/ppermute | solution.py:58
  8.6 8.5 %collective-permute-start.1 = (bf16[16,3712]{1,0:T(8,128)(2,1)S(1)}, bf16[16,3712]{1,0:T(8,128)(2,1)S(1)}, u32[]{:S(2)}, u32[]{:S(2)}) collective-permute-start(bf16[16,3712]{1,0:T(8,128)(2,1)S(1)} %get-tuple-element.102.refs_0_), channel_id=1, source_target_pairs={{0,5},{1,12},{4,9},{5,0},{8,13},{9,4},{12,1},{13,8},{16,29},{17,20... | collective-permute-start | bytes 356360 | tf_op jit(solution)/shard_map/ppermute | solution.py:35
  11.5 9.9 %collective-permute-start.3 = (bf16[16,3712]{1,0:T(8,128)(2,1)S(1)}, bf16[16,3712]{1,0:T(8,128)(2,1)S(1)}, u32[]{:S(2)}, u32[]{:S(2)}) collective-permute-start(bf16[16,3712]{1,0:T(8,128)(2,1)S(1)} %get-tuple-element.102.refs_0_), channel_id=1, source_target_pairs={{0,8},{1,9},{4,12},{5,13},{8,0},{9,1},{12,4},{13,5},{16,24},{17,25... | collective-permute-start | bytes 356360 | tf_op jit(solution)/shard_map/ppermute | solution.py:35
  12.9 8.5 %collective-permute-start.4 = (bf16[16,3712]{1,0:T(8,128)(2,1)S(1)}, bf16[16,3712]{1,0:T(8,128)(2,1)S(1)}, u32[]{:S(2)}, u32[]{:S(2)}) collective-permute-start(bf16[16,3712]{1,0:T(8,128)(2,1)S(1)} %get-tuple-element.106.refs_4_), channel_id=1, source_target_pairs={{0,17},{1,48},{4,53},{5,20},{8,25},{9,56},{12,61},{13,28},{16,33},... | collective-permute-start | bytes 356360 | tf_op jit(solution)/shard_map/ppermute | solution.py:35
  17.2 7.7 %collective-permute-start.6 = (bf16[16,3712]{1,0:T(8,128)(2,1)S(1)}, bf16[16,3712]{1,0:T(8,128)(2,1)S(1)}, u32[]{:S(2)}, u32[]{:S(2)}) collective-permute-start(bf16[16,3712]{1,0:T(8,128)(2,1)S(1)} %get-tuple-element.106.refs_4_), channel_id=1, source_target_pairs={{0,32},{1,33},{4,36},{5,37},{8,40},{9,41},{12,44},{13,45},{16,48},... | collective-permute-start | bytes 356360 | tf_op jit(solution)/shard_map/ppermute | solution.py:35
  24.9 9.4 %collective-permute-start.7 = (bf16[64,3712]{1,0:T(8,128)(2,1)S(1)}, bf16[64,3712]{1,0:T(8,128)(2,1)S(1)}, u32[]{:S(2)}, u32[]{:S(2)}) collective-permute-start(bf16[64,3712]{1,0:T(8,128)(2,1)S(1)} %get-tuple-element.110.refs_0_), channel_id=1, source_target_pairs={{0,17},{1,48},{4,53},{5,20},{8,25},{9,56},{12,61},{13,28},{16,33},... | collective-permute-start | bytes 1425416 | tf_op jit(solution)/shard_map/ppermute | solution.py:35
  27.3 9.3 %collective-permute-start.8 = (bf16[64,3712]{1,0:T(8,128)(2,1)S(1)}, bf16[64,3712]{1,0:T(8,128)(2,1)S(1)}, u32[]{:S(2)}, u32[]{:S(2)}) collective-permute-start(bf16[64,3712]{1,0:T(8,128)(2,1)S(1)} %get-tuple-element.111.refs_2_), channel_id=1, source_target_pairs={{0,5},{1,12},{4,9},{5,0},{8,13},{9,4},{12,1},{13,8},{16,29},{17,20... | collective-permute-start | bytes 1425416 | tf_op jit(solution)/shard_map/ppermute | solution.py:35
  36.8 13.5 %collective-permute-start.10 = (bf16[128,3712]{1,0:T(8,128)(2,1)S(1)}, bf16[128,3712]{1,0:T(8,128)(2,1)S(1)}, u32[]{:S(2)}, u32[]{:S(2)}) collective-permute-start(bf16[128,3712]{1,0:T(8,128)(2,1)S(1)} %get-tuple-element.113.a_ref), channel_id=1, source_target_pairs={{0,49},{1,16},{4,21},{5,52},{8,57},{9,24},{12,29},{13,60},{16,1},{... | collective-permute-start | bytes 2850824 | tf_op jit(solution)/shard_map/ppermute | solution.py:35
  37.3 13.5 %collective-permute-start.11 = (bf16[128,3712]{1,0:T(8,128)(2,1)S(1)}, bf16[128,3712]{1,0:T(8,128)(2,1)S(1)}, u32[]{:S(2)}, u32[]{:S(2)}) collective-permute-start(bf16[128,3712]{1,0:T(8,128)(2,1)S(1)} %get-tuple-element.114.b_ref), channel_id=1, source_target_pairs={{0,13},{1,4},{4,1},{5,8},{8,5},{9,12},{12,9},{13,0},{16,21},{17,28... | collective-permute-start | bytes 2850824 | tf_op jit(solution)/shard_map/ppermute | solution.py:35
  37.3 24.1 %collective-permute-start.13 = (bf16[128,3712]{1,0:T(8,128)(2,1)S(1)}, bf16[128,3712]{1,0:T(8,128)(2,1)S(1)}, u32[]{:S(2)}, u32[]{:S(2)}) collective-permute-start(bf16[128,3712]{1,0:T(8,128)(2,1)S(1)} %get-tuple-element.113.a_ref), channel_id=1, source_target_pairs={{0,1},{1,0},{2,3},{3,2},{4,5},{5,4},{6,7},{7,6},{8,9},{9,8},{10,11... | collective-permute-start | bytes 2850824 | tf_op jit(solution)/shard_map/ppermute | solution.py:58
  37.8 23.6 %collective-permute-start.14 = (bf16[128,3712]{1,0:T(8,128)(2,1)S(1)}, bf16[128,3712]{1,0:T(8,128)(2,1)S(1)}, u32[]{:S(2)}, u32[]{:S(2)}) collective-permute-start(bf16[128,3712]{1,0:T(8,128)(2,1)S(1)} %get-tuple-element.114.b_ref), channel_id=1, source_target_pairs={{0,1},{1,0},{2,3},{3,2},{4,5},{5,4},{6,7},{7,6},{8,9},{9,8},{10,11... | collective-permute-start | bytes 2850824 | tf_op jit(solution)/shard_map/ppermute | solution.py:58
  61.4 13.8 %collective-permute-start.24 = (bf16[128,3712]{1,0:T(8,128)(2,1)S(1)}, bf16[128,3712]{1,0:T(8,128)(2,1)S(1)}, u32[]{:S(2)}, u32[]{:S(2)}) collective-permute-start(bf16[128,3712]{1,0:T(8,128)(2,1)S(1)} %collective-permute-done.10.a_ref), channel_id=1, source_target_pairs={{0,1},{1,0},{2,3},{3,2},{4,5},{5,4},{6,7},{7,6},{8,9},{9,8},{10,11... | collective-permute-start | bytes 2850824 | tf_op jit(solution)/shard_map/ppermute | solution.py:58
  61.5 13.7 %collective-permute-start.25 = (bf16[128,3712]{1,0:T(8,128)(2,1)S(1)}, bf16[128,3712]{1,0:T(8,128)(2,1)S(1)}, u32[]{:S(2)}, u32[]{:S(2)}) collective-permute-start(bf16[128,3712]{1,0:T(8,128)(2,1)S(1)} %collective-permute-done.11.b_ref), channel_id=1, source_target_pairs={{0,1},{1,0},{2,3},{3,2},{4,5},{5,4},{6,7},{7,6},{8,9},{9,8},{10,11... | collective-permute-start | bytes 2850824 | tf_op jit(solution)/shard_map/ppermute | solution.py:58
  68.3 7.5 %collective-permute-start.21 = (f32[8,512]{1,0:T(8,128)S(1)}, f32[8,512]{1,0:T(8,128)S(1)}, u32[]{:S(2)}, u32[]{:S(2)}) collective-permute-start(f32[8,512]{1,0:T(8,128)S(1)} %shard_map.94.refs_0_), channel_id=1, source_target_pairs={{0,65},{1,66},{4,71},{5,68},{8,73},{9,74},{12,79},{13,76},{16,83},... | collective-permute-start | bytes 49160 | tf_op jit(solution)/shard_map/ppermute | solution.py:35
  81.8 14.1 %collective-permute-start.26 = (bf16[128,3584]{1,0:T(8,128)(2,1)S(1)}, bf16[128,3584]{1,0:T(8,128)(2,1)S(1)}, u32[]{:S(2)}, u32[]{:S(2)}) collective-permute-start(bf16[128,3584]{1,0:T(8,128)(2,1)S(1)} %get-tuple-element.147), channel_id=1, source_target_pairs={{0,49},{1,16},{4,21},{5,52},{8,57},{9,24},{12,29},{13,60},{16,1},{... | collective-permute-start | bytes 2752520 | tf_op jit(solution)/shard_map/ppermute | solution.py:35
  83.9 13.1 %collective-permute-start.27 = (bf16[128,3584]{1,0:T(8,128)(2,1)S(1)}, bf16[128,3584]{1,0:T(8,128)(2,1)S(1)}, u32[]{:S(2)}, u32[]{:S(2)}) collective-permute-start(bf16[128,3584]{1,0:T(8,128)(2,1)S(1)} %get-tuple-element.148), channel_id=1, source_target_pairs={{0,13},{1,4},{4,1},{5,8},{8,5},{9,12},{12,9},{13,0},{16,21},{17,28... | collective-permute-start | bytes 2752520 | tf_op jit(solution)/shard_map/ppermute | solution.py:35
  89.0 6.8 %collective-permute-start.30 = (f32[8,128]{1,0:T(8,128)S(1)}, f32[8,128]{1,0:T(8,128)S(1)}, u32[]{:S(2)}, u32[]{:S(2)}) collective-permute-start(f32[8,128]{1,0:T(8,128)S(1)} %get-tuple-element.161), channel_id=1, source_target_pairs={{0,1},{1,0},{2,3},{3,2},{4,5},{5,4},{6,7},{7,6},{8,9},{9,8},{10,11... | collective-permute-start | bytes 12296 | tf_op jit(solution)/shard_map/ppermute | solution.py:58
  97.5 9.2 %collective-permute-start.31 = (bf16[64,3584]{1,0:T(8,128)(2,1)S(1)}, bf16[64,3584]{1,0:T(8,128)(2,1)S(1)}, u32[]{:S(2)}, u32[]{:S(2)}) collective-permute-start(bf16[64,3584]{1,0:T(8,128)(2,1)S(1)} %get-tuple-element.167), channel_id=1, source_target_pairs={{0,17},{1,48},{4,53},{5,20},{8,25},{9,56},{12,61},{13,28},{16,33},... | collective-permute-start | bytes 1376264 | tf_op jit(solution)/shard_map/ppermute | solution.py:35
  98.8 9.1 %collective-permute-start.32 = (bf16[64,3584]{1,0:T(8,128)(2,1)S(1)}, bf16[64,3584]{1,0:T(8,128)(2,1)S(1)}, u32[]{:S(2)}, u32[]{:S(2)}) collective-permute-start(bf16[64,3584]{1,0:T(8,128)(2,1)S(1)} %get-tuple-element.168), channel_id=1, source_target_pairs={{0,5},{1,12},{4,9},{5,0},{8,13},{9,4},{12,1},{13,8},{16,29},{17,20... | collective-permute-start | bytes 1376264 | tf_op jit(solution)/shard_map/ppermute | solution.py:35
  108.1 9.7 %collective-permute-start.33 = (bf16[16,3584]{1,0:T(8,128)(2,1)S(1)}, bf16[16,3584]{1,0:T(8,128)(2,1)S(1)}, u32[]{:S(2)}, u32[]{:S(2)}) collective-permute-start(bf16[16,3584]{1,0:T(8,128)(2,1)S(1)} %get-tuple-element.173), channel_id=1, source_target_pairs={{0,5},{1,12},{4,9},{5,0},{8,13},{9,4},{12,1},{13,8},{16,29},{17,20... | collective-permute-start | bytes 344072 | tf_op jit(solution)/shard_map/ppermute | solution.py:35
  113.3 7.5 %collective-permute-start.34 = (bf16[16,3584]{1,0:T(8,128)(2,1)S(1)}, bf16[16,3584]{1,0:T(8,128)(2,1)S(1)}, u32[]{:S(2)}, u32[]{:S(2)}) collective-permute-start(bf16[16,3584]{1,0:T(8,128)(2,1)S(1)} %get-tuple-element.174), channel_id=1, source_target_pairs={{0,17},{1,48},{4,53},{5,20},{8,25},{9,56},{12,61},{13,28},{16,33},... | collective-permute-start | bytes 344072 | tf_op jit(solution)/shard_map/ppermute | solution.py:35
  113.7 7.1 %collective-permute-start.35 = (bf16[16,3584]{1,0:T(8,128)(2,1)S(1)}, bf16[16,3584]{1,0:T(8,128)(2,1)S(1)}, u32[]{:S(2)}, u32[]{:S(2)}) collective-permute-start(bf16[16,3584]{1,0:T(8,128)(2,1)S(1)} %get-tuple-element.175), channel_id=1, source_target_pairs={{0,13},{1,4},{4,1},{5,8},{8,5},{9,12},{12,9},{13,0},{16,21},{17,28... | collective-permute-start | bytes 344072 | tf_op jit(solution)/shard_map/ppermute | solution.py:35
  113.9 6.9 %collective-permute-start.36 = (bf16[16,3584]{1,0:T(8,128)(2,1)S(1)}, bf16[16,3584]{1,0:T(8,128)(2,1)S(1)}, u32[]{:S(2)}, u32[]{:S(2)}) collective-permute-start(bf16[16,3584]{1,0:T(8,128)(2,1)S(1)} %get-tuple-element.176), channel_id=1, source_target_pairs={{0,49},{1,16},{4,21},{5,52},{8,57},{9,24},{12,29},{13,60},{16,1},{... | collective-permute-start | bytes 344072 | tf_op jit(solution)/shard_map/ppermute | solution.py:35
  114.0 8.5 %collective-permute-start.37 = (bf16[16,3584]{1,0:T(8,128)(2,1)S(1)}, bf16[16,3584]{1,0:T(8,128)(2,1)S(1)}, u32[]{:S(2)}, u32[]{:S(2)}) collective-permute-start(bf16[16,3584]{1,0:T(8,128)(2,1)S(1)} %get-tuple-element.177), channel_id=1, source_target_pairs={{0,8},{1,9},{4,12},{5,13},{8,0},{9,1},{12,4},{13,5},{16,24},{17,25... | collective-permute-start | bytes 344072 | tf_op jit(solution)/shard_map/ppermute | solution.py:35
  (20 other events, 85.0 us)
where the time goes:
time: 134 us
  starting transfers between devices  59.2 us (44%)
  waiting for transfers between devices  32.8 us (24%)
  Pallas kernels  31.5 us (24%)
  between operations  4.68 us (3%)
  other arithmetic  2.14 us (2%)
  matrix products  2.14 us (2%)
    ppermute x34, starting transfers between devices, moved(): return lax.ppermute(value, TOK_VOC, pairs)  55 us
    pallas_call x20, Pallas kernels, call(): pl.pallas_call(kernel, out_shape=shapes, in_specs=in_specs, out_specs=out...  31.5 us
    ppermute x34, waiting for transfers between devices, moved(): return lax.ppermute(value, TOK_VOC, pairs)  30.6 us
    ppermute x9, starting transfers between devices, swap_core(): return lax.ppermute(value, CORE, [(0, 1), (1, 0)])  4.23 us
  transfers between devices with their start and end apart: 43, of which 22 were waited for; matrix products, arithmetic and copies ran while one was open for 4% of the time, Pallas kernels for 20%

commit v1 on v0

--- a/solution.py
+++ b/solution.py
@@ -42,6 +42,17 @@
         at = {"y": y, "z": z, "x": x}
         at[ring] ^= xor
         return at["y"], at["z"], at["x"], group_of(group, at["y"], at["z"], at["x"])
+
+    return moved(value, target)
+
+
+def along(value, own, step):
+    def target(y, z, x, c):
+        group = group_of(c, y, z, x)
+        xor = XORS[group][step]
+        even = (y % 2 == 0) == own
+        to_z, to_x = (z, x ^ xor) if even else (z ^ xor, x)
+        return y, to_z, to_x, group_of(group, y, to_z, to_x)
 
     return moved(value, target)
 
@@ -166,21 +177,34 @@
     )[0]
 
 
-def joined(*groups, after=()):
+def joined(*groups, after=(), parity=None):
     sizes = [len(g) for g in groups]
     pieces = [p for g in groups for p in g]
+    n = len(pieces)
 
     def kernel(*refs):
-        ins, outs = list(refs[: len(pieces)]), refs[len(refs) - len(groups) :]
-        for out_ref, size in zip(outs, sizes):
-            at = 0
-            for _ in range(size):
-                ref = ins.pop(0)
-                out_ref[at : at + ref.shape[0]] = ref[...]
-                at += ref.shape[0]
+        outs = refs[len(refs) - len(groups) :]
+
+        def put(outs):
+            ins = list(refs[:n])
+            for out_ref, size in zip(outs, sizes):
+                at = 0
+                for _ in range(size):
+                    ref = ins.pop(0)
+                    out_ref[at : at + ref.shape[0]] = ref[...]
+                    at += ref.shape[0]
+
+        if parity is None:
+            put(outs)
+        else:
+            pl.when(refs[n][1] == 0)(lambda: put(outs))
+            pl.when(refs[n][1] != 0)(lambda: put(outs[::-1]))
 
     outs = [((sum(p.shape[0] for p in g), g[0].shape[1]), g[0].dtype) for g in groups]
-    return call(kernel, [*pieces, *after], outs, mib=4)
+    operands, specs = [*pieces, *after], [VMEM] * (n + len(after))
+    if parity is not None:
+        operands, specs = [*operands, parity], [*specs, SMEM]
+    return call(kernel, operands, outs, in_specs=specs, mib=4)
 
 
 def turned(a, b, width):
@@ -196,49 +220,56 @@
     return call(kernel, [a, b], [((width, 2 * rows), a.dtype)], flops=10**9)[0]
 
 
-def added(groups, blocks):
+def added(groups, blocks, parity=None):
     sizes = [len(g) for g in groups]
     parts = [p for g in groups for p in g]
+    n = len(parts)
 
     def kernel(*refs):
-        ins, outs = list(refs[: len(parts)]), list(refs[len(parts) :])
-        for size in sizes:
-            terms = [ins.pop(0) for _ in range(size)]
-            cut = terms[0].shape[0] // blocks
-            for k in range(blocks):
-                at = slice(k * cut, (k + 1) * cut)
-                total = sum(t[at].astype(jnp.float32) for t in terms[1:])
-                outs.pop(0)[...] = (total + terms[0][at].astype(jnp.float32)).astype(jnp.bfloat16)
+        outs = refs[len(refs) - blocks * len(groups) :]
+
+        def put(outs):
+            ins, outs = list(refs[:n]), list(outs)
+            for size in sizes:
+                terms = [ins.pop(0) for _ in range(size)]
+                cut = terms[0].shape[0] // blocks
+                for k in range(blocks):
+                    at = slice(k * cut, (k + 1) * cut)
+                    total = sum(t[at].astype(jnp.float32) for t in terms)
+                    outs.pop(0)[...] = total.astype(jnp.bfloat16)
+
+        if parity is None:
+            put(outs)
+        else:
+            pl.when(refs[n][1] == 0)(lambda: put(outs))
+            pl.when(refs[n][1] != 0)(lambda: put(outs[blocks:] + outs[:blocks]))
 
     outs = [
         ((g[0].shape[0] // blocks, g[0].shape[1]), jnp.bfloat16) for g in groups for _ in range(blocks)
     ]
-    return call(kernel, parts, outs, mib=4)
-
-
-def added_by_place(groups, spot):
-    sizes = [len(g) for g in groups]
-    parts = [p for g in groups for p in g]
+    operands, specs = parts, [VMEM] * n
+    if parity is not None:
+        operands, specs = [*parts, parity], [*specs, SMEM]
+    return call(kernel, operands, outs, in_specs=specs, mib=4)
+
+
+def added_by_place(parts, spot, steps, after=()):
     rows, width = parts[0].shape
 
     def kernel(spot_ref, *refs):
-        ins, outs, sums = list(refs[: len(parts)]), refs[len(parts) : -1], refs[-1]
-        for k, size in enumerate(sizes):
-            terms = [ins.pop(0) for _ in range(size)]
-            sums[k * rows : (k + 1) * rows] = sum(t[...].astype(jnp.float32) for t in terms)
-        for k, out_ref in enumerate(outs):
-            step = 0 if k == 0 else jnp.where(spot_ref[0] == 0, XORS[0][k - 1], XORS[1][k - 1])
-            y = (spot_ref[2] * 2 + spot_ref[1]) ^ step
-            at = pl.multiple_of(((y & 1) * 2 + (y >> 1)) * 8, 8)
+        ins, outs, sums = refs[: len(parts)], refs[len(parts) + len(after) : -1], refs[-1]
+        sums[...] = sum(t[...].astype(jnp.float32) for t in ins)
+        for k, out_ref in zip(steps, outs):
+            xor = 0 if k is None else jnp.where(spot_ref[0] == 0, XORS[0][k], XORS[1][k])
+            at = pl.multiple_of((spot_ref[2] ^ (xor >> 1)) * 8, 8)
             out_ref[...] = sums[pl.ds(at, 8), :].astype(jnp.bfloat16)
 
-    blocks = len(groups) * rows // 8
     return call(
         kernel,
-        [spot, *parts],
-        [((8, width), jnp.bfloat16)] * blocks,
-        in_specs=[SMEM] + [VMEM] * len(parts),
-        scratch=[pltpu.VMEM((len(groups) * rows, width), jnp.float32)],
+        [spot, *parts, *after],
+        [((8, width), jnp.bfloat16)] * len(steps),
+        in_specs=[SMEM] + [VMEM] * (len(parts) + len(after)),
+        scratch=[pltpu.VMEM((rows, width), jnp.float32)],
         mib=4,
     )
 
@@ -490,16 +521,14 @@
         other, teacher_send, spot, places, own_group
     )
     teacher_in = swap_core(teacher_send)
-    near_a = jnp.where(y_low == 0, block, other)
-    near_b = jnp.where(y_low == 0, other, block)
-
-    pieces_a, pieces_b = [near_a], [near_b]
+    own, across = [block], [other]
     for step in range(3):
-        pieces_a.append(swap(near_a, "x", step))
-        pieces_b.append(swap(near_b, "z", step))
+        own.append(along(block, True, step))
+    for step in range(3):
+        across.append(along(other, False, step))
     teacher = jnp.dot(one_hot(token, tokens, bf16), teacher_logits)
-    *pieces, teacher = together(*pieces_a, *pieces_b, teacher)
-    near_a, near_b = joined(pieces[:4], pieces[4:])
+    *pieces, teacher = together(*own, *across, teacher)
+    near_a, near_b = joined(pieces[:4], pieces[4:], parity=spot)
 
     far_a, far_b = swap(near_a, "z", 0), swap(near_b, "x", 0)
     heads, mark = side_by_side(student_head, head_in)
@@ -545,18 +574,20 @@
     a_in, b_in = swap(send_a, "z", 0), swap(send_b, "x", 0)
     head_grad = head_gradient(states, all_d, range(4, width // 512), head_grad)
     a_in, b_in, head_grad = together(a_in, b_in, head_grad)
-    keep_a, *send_a, keep_b, to_1, to_2, to_3 = added(((keep_a, a_in), (keep_b, b_in)), 4)
-    arrived = [
-        swap(part, ring, step)
-        for step in range(3)
-        for part, ring in ((send_a[step], "x"), ((to_1, to_2, to_3)[step], "z"))
-    ]
+    *own, across, to_1, to_2, to_3 = added(((keep_a, a_in), (keep_b, b_in)), 4, spot)
+    across_in = []
+    for step, part in enumerate((to_1, to_2, to_3)):
+        across_in.append(along(part, False, step))
+    own_in = []
+    for step in range(3):
+        own_in.append(along(own[step + 1], True, step))
+    send = added_by_place((across, *across_in), spot, (0, 1))
+    arrived = [to_owner(part, step) for step, part in enumerate(send)]
+    keep, last = added_by_place((own[0], *own_in), spot, (None, 2), after=(send[0],))
+    keep, sums, other_sums = together(keep, sums, other_sums)
+    parts = [to_owner(keep), *arrived, to_owner(last, 2)]
     loss = (sums[0, 0] + other_sums[0, 0]) / (sums[1, 0] + other_sums[1, 0])
     sampled_ratio = jnp.where(own_group, sums[2, :8], other_sums[2, :8])
-    *arrived, loss, sampled_ratio = together(*arrived, loss, sampled_ratio)
-    keep, *send = added_by_place(((keep_a, *arrived[0::2]), (keep_b, *arrived[1::2])), spot)
-    arrived = [to_owner(part, step) for step, part in enumerate(send)]
-    parts = [to_owner(keep), *arrived]
     hidden_grad = sum(p.astype(f32) for p in parts).astype(bf16)
     return (loss, sampled_ratio, hidden_grad, head_grad)
 

time: 134 us -> 131 us (0.978)
  waiting for transfers between devices: 32.8 us -> 27.8 us
  Pallas kernels: 31.5 us -> 33 us
    ppermute x34, waiting for transfers between devices: 30.6 us -> 25.9 us  [moved(): return lax.ppermute(value, TOK_VOC, pairs)]
    pallas_call x20 -> x21, Pallas kernels: 31.5 us -> 33 us  [call(): pl.pallas_call(kernel, out_shape=shapes, in_specs=in_specs, out_specs=out...]
  transfers between devices with their start and end apart: 43 -> 43, of which waited for: 22 -> 22; matrix products, arithmetic and copies ran while one was open for 4% -> 3% of each run, Pallas kernels for 20% -> 22%
where the time goes in v1:
time: 131 us; the launch traced here: 130 us
  starting transfers between devices  60 us (46%)
  Pallas kernels  33 us (25%)
  waiting for transfers between devices  27.8 us (21%)
  between operations  4.71 us (4%)
  matrix products  2.14 us (2%)
  other arithmetic  2.12 us (2%)
    ppermute x34, starting transfers between devices, moved(): return lax.ppermute(value, TOK_VOC, pairs)  54.8 us
    pallas_call x21, Pallas kernels, call(): pl.pallas_call(kernel, out_shape=shapes, in_specs=in_specs, out_specs=out...  33 us
    ppermute x34, waiting for transfers between devices, moved(): return lax.ppermute(value, TOK_VOC, pairs)  25.9 us
    ppermute x9, starting transfers between devices, swap_core(): return lax.ppermute(value, CORE, [(0, 1), (1, 0)])  5.16 us
  transfers between devices with their start and end apart: 43, of which 22 were waited for; matrix products, arithmetic and copies ran while one was open for 3% of the time, Pallas kernels for 22%

profile of v1, /device:TPU:1, one launch (start us, length us, event | category | flops | bytes accessed | tf_op | source)
XLA Modules:
  0.0 130.3 jit_solution(1494791176037920926)
XLA Ops:
  3.0 2.9 %collective-permute-start = (bf16[16,3712]{1,0:T(8,128)(2,1)S(1)}, bf16[16,3712]{1,0:T(8,128)(2,1)S(1)}, u32[]{:S(2)}, u32[]{:S(2)}) collective-permute-start(bf16[16,3712]{1,0:T(8,128)(2,1)S(1)} %shard_map.84.refs_0_), channel_id=1, source_target_pairs={{0,65},{1,66},{4,71},{5,68},{8,73},{9,74},{12,79},{13,76},{16,83},... | collective-permute-start | bytes 356360 | tf_op jit(solution)/shard_map/ppermute | solution.py:35
  6.0 2.8 %collective-permute-start.1 = (bf16[16,3712]{1,0:T(8,128)(2,1)S(1)}, bf16[16,3712]{1,0:T(8,128)(2,1)S(1)}, u32[]{:S(2)}, u32[]{:S(2)}) collective-permute-start(bf16[16,3712]{1,0:T(8,128)(2,1)S(1)} %shard_map.84.refs_0_), channel_id=1, source_target_pairs={{0,5},{1,12},{4,9},{5,0},{8,13},{9,4},{12,1},{13,8},{16,29},{17,20... | collective-permute-start | bytes 356360 | tf_op jit(solution)/shard_map/ppermute | solution.py:35
  12.1 4.4 %collective-permute-start.4 = (bf16[16,3712]{1,0:T(8,128)(2,1)S(1)}, bf16[16,3712]{1,0:T(8,128)(2,1)S(1)}, u32[]{:S(2)}, u32[]{:S(2)}) collective-permute-start(bf16[16,3712]{1,0:T(8,128)(2,1)S(1)} %collective-permute-done.refs_4_), channel_id=1, source_target_pairs={{0,17},{1,48},{4,53},{5,20},{8,25},{9,56},{12,61},{13,28},{16,33},... | collective-permute-start | bytes 356360 | tf_op jit(solution)/shard_map/ppermute | solution.py:35
  23.3 2.6 %collective-permute-start.7 = (bf16[64,3712]{1,0:T(8,128)(2,1)S(1)}, bf16[64,3712]{1,0:T(8,128)(2,1)S(1)}, u32[]{:S(2)}, u32[]{:S(2)}) collective-permute-start(bf16[64,3712]{1,0:T(8,128)(2,1)S(1)} %get-tuple-element.105.refs_0_), channel_id=1, source_target_pairs={{0,17},{1,48},{4,53},{5,20},{8,25},{9,56},{12,61},{13,28},{16,33},... | collective-permute-start | bytes 1425416 | tf_op jit(solution)/shard_map/ppermute | solution.py:35
  27.8 3.7 %shard_map.86 = (bf16[3584,1280]{1,0:T(8,128)(2,1)S(1)}, f32[8,128]{1,0:T(8,128)S(1)}) custom-call(bf16[3584,640]{1,0:T(8,128)(2,1)} %h_ref.1, bf16[3584,640]{1,0:T(8,128)(2,1)} %collective-permute-done.9.g_ref), custom_call_target="tpu_custom_call" | custom-call | flops 4000000000 | bytes 1000000 | tf_op jit(solution)/shard_map/pallas_call | solution.py:121
  32.6 2.5 %collective-permute-done.8.refs_3_ = bf16[64,3712]{1,0:T(8,128)(2,1)S(1)} collective-permute-done((bf16[64,3712]{1,0:T(8,128)(2,1)S(1)}, bf16[64,3712]{1,0:T(8,128)(2,1)S(1)}, u32[]{:S(2)}, u32[]{:S(2)}) %collective-permute-start.8) | collective-permute-done | bytes 475168 | tf_op jit(solution)/shard_map/ppermute | solution.py:35
  37.9 3.8 %shard_map.88 = (f32[256,1280]{1,0:T(8,128)S(1)}, f32[8,512]{1,0:T(8,128)S(1)}) custom-call(s32[4]{0:T(128)S(1)} %pad_add_fusion.refs_8_.spot_ref.refs_4_, bf16[128,3712]{1,0:T(8,128)(2,1)S(1)} %get-tuple-element.108.a_ref, bf16[128,3712]{1,0:T(8,128)(2,1)S(1)} %get-tuple-element.109.b_ref, bf16[3584,1280]{1,0:T(8,128)(2,1)S(1)} %get-tuple-element.110.h_ref, ...), custom_call_target="tpu_custom_call" | custom-call | flops 2348810240 | bytes 1000000 | tf_op jit(solution)/shard_map/pallas_call | solution.py:121
  41.8 6.8 %collective-permute-done.10.a_ref = bf16[128,3712]{1,0:T(8,128)(2,1)S(1)} collective-permute-done((bf16[128,3712]{1,0:T(8,128)(2,1)S(1)}, bf16[128,3712]{1,0:T(8,128)(2,1)S(1)}, u32[]{:S(2)}, u32[]{:S(2)}) %collective-permute-start.10) | collective-permute-done | bytes 950304 | tf_op jit(solution)/shard_map/ppermute | solution.py:35
  48.6 3.8 %shard_map.90 = (f32[256,1280]{1,0:T(8,128)S(1)}, f32[8,512]{1,0:T(8,128)S(1)}) custom-call(s32[4]{0:T(128)S(1)} %pad_add_fusion.refs_8_.spot_ref.refs_4_, bf16[128,3712]{1,0:T(8,128)(2,1)S(1)} %collective-permute-done.10.a_ref, bf16[128,3712]{1,0:T(8,128)(2,1)S(1)} %collective-permute-done.11.b_ref, bf16[3584,1280]{1,0:T(8,128)(2,1)S(1)} %get-tuple-element.110.h_ref, ...), custom_call_target="tpu_custom_call" | custom-call | flops 2348810240 | bytes 1000000 | tf_op jit(solution)/shard_map/pallas_call | solution.py:121
  52.5 2.5 %collective-permute-start.15 = (f32[8,512]{1,0:T(8,128)S(1)}, f32[8,512]{1,0:T(8,128)S(1)}, u32[]{:S(2)}, u32[]{:S(2)}) collective-permute-start(f32[8,512]{1,0:T(8,128)S(1)} %get-tuple-element.121.refs_0_), channel_id=1, source_target_pairs={{0,5},{1,12},{4,9},{5,0},{8,13},{9,4},{12,1},{13,8},{16,29},{17,20... | collective-permute-start | bytes 49160 | tf_op jit(solution)/shard_map/ppermute | solution.py:35
  60.1 2.1 %collective-permute-start.18 = (f32[8,512]{1,0:T(8,128)S(1)}, f32[8,512]{1,0:T(8,128)S(1)}, u32[]{:S(2)}, u32[]{:S(2)}) collective-permute-start(f32[8,512]{1,0:T(8,128)S(1)} %shard_map.92.refs_0_), channel_id=1, source_target_pairs={{0,17},{1,48},{4,53},{5,20},{8,25},{9,56},{12,61},{13,28},{16,33},... | collective-permute-start | bytes 49160 | tf_op jit(solution)/shard_map/ppermute | solution.py:35
  62.2 2.0 %collective-permute-start.20 = (f32[8,512]{1,0:T(8,128)S(1)}, f32[8,512]{1,0:T(8,128)S(1)}, u32[]{:S(2)}, u32[]{:S(2)}) collective-permute-start(f32[8,512]{1,0:T(8,128)S(1)} %shard_map.92.refs_0_), channel_id=1, source_target_pairs={{0,32},{1,33},{4,36},{5,37},{8,40},{9,41},{12,44},{13,45},{16,48},... | collective-permute-start | bytes 49160 | tf_op jit(solution)/shard_map/ppermute | solution.py:35
  66.3 2.7 %collective-permute-start.21 = (f32[8,512]{1,0:T(8,128)S(1)}, f32[8,512]{1,0:T(8,128)S(1)}, u32[]{:S(2)}, u32[]{:S(2)}) collective-permute-start(f32[8,512]{1,0:T(8,128)S(1)} %shard_map.94.refs_0_), channel_id=1, source_target_pairs={{0,65},{1,66},{4,71},{5,68},{8,73},{9,74},{12,79},{13,76},{16,83},... | collective-permute-start | bytes 49160 | tf_op jit(solution)/shard_map/ppermute | solution.py:35
  73.8 3.1 %shard_map.97 = (bf16[128,3584]{1,0:T(8,128)(2,1)S(1)}, bf16[128,3584]{1,0:T(8,128)(2,1)S(1)}, bf16[256,640]{1,0:T(8,128)(2,1)S(1)}, bf16[256,640]{1,0:T(8,128)(2,1)S(1)}) custom-call(f32[256,1280]{1,0:T(8,128)S(1)} %get-tuple-element.119.s_ref, f32[8,512]{1,0:T(8,128)S(1)} %get-tuple-element.145.c_ref, bf16[3584,1280]{1,0:T(8,128)(2,1)S(1)} %get-tuple-element.110.h_ref, ...), custom_call_target="tpu_custom_call" | custom-call | flops 2348810240 | bytes 1000000 | tf_op jit(solution)/shard_map/pallas_call | solution.py:121
  76.9 2.9 %collective-permute-start.26 = (bf16[128,3584]{1,0:T(8,128)(2,1)S(1)}, bf16[128,3584]{1,0:T(8,128)(2,1)S(1)}, u32[]{:S(2)}, u32[]{:S(2)}) collective-permute-start(bf16[128,3584]{1,0:T(8,128)(2,1)S(1)} %get-tuple-element.142), channel_id=1, source_target_pairs={{0,49},{1,16},{4,21},{5,52},{8,57},{9,24},{12,29},{13,60},{16,1},{... | collective-permute-start | bytes 2752520 | tf_op jit(solution)/shard_map/ppermute | solution.py:35
  80.6 3.1 %shard_map.98 = (bf16[128,3584]{1,0:T(8,128)(2,1)S(1)}, bf16[128,3584]{1,0:T(8,128)(2,1)S(1)}, bf16[256,640]{1,0:T(8,128)(2,1)S(1)}, bf16[256,640]{1,0:T(8,128)(2,1)S(1)}) custom-call(f32[256,1280]{1,0:T(8,128)S(1)} %get-tuple-element.144.s_ref, f32[8,512]{1,0:T(8,128)S(1)} %get-tuple-element.145.c_ref, bf16[3584,1280]{1,0:T(8,128)(2,1)S(1)} %get-tuple-element.110.h_ref, ...), custom_call_target="tpu_custom_call" | custom-call | flops 2348810240 | bytes 1000000 | tf_op jit(solution)/shard_map/pallas_call | solution.py:121
  86.7 5.2 %shard_map.99.refs_8_ = bf16[3584,640]{1,0:T(8,128)(2,1)} custom-call(bf16[3584,256]{1,0:T(8,128)(2,1)S(1)} %shard_map.89.refs_0_, bf16[3584,256]{1,0:T(8,128)(2,1)S(1)} %shard_map.91.refs_1_, bf16[3584,256]{1,0:T(8,128)(2,1)S(1)} %shard_map.93.refs_2_, bf16[3584,256]{1,0:T(8,128)(2,1)S(1)} %shard_map.95.refs_3_, ...), custom_call_target="tpu_custom_call" | custom-call | flops 2684354560 | bytes 1000000 | tf_op jit(solution)/shard_map/pallas_call | solution.py:121
  96.2 3.6 %shard_map.101 = bf16[3584,640]{1,0:T(8,128)(2,1)} custom-call(bf16[3584,256]{1,0:T(8,128)(2,1)S(1)} %shard_map.89.refs_0_, bf16[3584,256]{1,0:T(8,128)(2,1)S(1)} %shard_map.91.refs_1_, bf16[3584,256]{1,0:T(8,128)(2,1)S(1)} %shard_map.93.refs_2_, bf16[3584,256]{1,0:T(8,128)(2,1)S(1)} %shard_map.95.refs_3_, ...), custom_call_target="tpu_custom_call", output_to_operand_aliasing={{}: (8, {})} | custom-call | flops 2013265920 | bytes 1000000 | tf_op jit(solution)/shard_map/pallas_call | solution.py:121
  99.8 2.7 %collective-permute-done.31.refs_1_ = bf16[64,3584]{1,0:T(8,128)(2,1)S(1)} collective-permute-done((bf16[64,3584]{1,0:T(8,128)(2,1)S(1)}, bf16[64,3584]{1,0:T(8,128)(2,1)S(1)}, u32[]{:S(2)}, u32[]{:S(2)}) %collective-permute-start.31) | collective-permute-done | bytes 458784 | tf_op jit(solution)/shard_map/ppermute | solution.py:35
  104.2 2.1 %collective-permute-start.36 = (bf16[16,3584]{1,0:T(8,128)(2,1)S(1)}, bf16[16,3584]{1,0:T(8,128)(2,1)S(1)}, u32[]{:S(2)}, u32[]{:S(2)}) collective-permute-start(bf16[16,3584]{1,0:T(8,128)(2,1)S(1)} %get-tuple-element.173), channel_id=1, source_target_pairs={{0,17},{1,48},{4,53},{5,20},{8,25},{9,56},{12,61},{13,28},{16,33},... | collective-permute-start | bytes 344072 | tf_op jit(solution)/shard_map/ppermute | solution.py:35
  106.3 2.1 %collective-permute-start.38 = (bf16[16,3584]{1,0:T(8,128)(2,1)S(1)}, bf16[16,3584]{1,0:T(8,128)(2,1)S(1)}, u32[]{:S(2)}, u32[]{:S(2)}) collective-permute-start(bf16[16,3584]{1,0:T(8,128)(2,1)S(1)} %get-tuple-element.175), channel_id=1, source_target_pairs={{0,32},{1,33},{4,36},{5,37},{8,40},{9,41},{12,44},{13,45},{16,48},... | collective-permute-start | bytes 344072 | tf_op jit(solution)/shard_map/ppermute | solution.py:35
  108.4 2.2 %collective-permute-start.33 = (bf16[16,3584]{1,0:T(8,128)(2,1)S(1)}, bf16[16,3584]{1,0:T(8,128)(2,1)S(1)}, u32[]{:S(2)}, u32[]{:S(2)}) collective-permute-start(bf16[16,3584]{1,0:T(8,128)(2,1)S(1)} %get-tuple-element.169), channel_id=1, source_target_pairs={{0,5},{1,12},{4,9},{5,0},{8,13},{9,4},{12,1},{13,8},{16,29},{17,20... | collective-permute-start | bytes 344072 | tf_op jit(solution)/shard_map/ppermute | solution.py:35
  113.7 3.3 %collective-permute-start.40 = (bf16[8,3584]{1,0:T(8,128)(2,1)S(1)}, bf16[8,3584]{1,0:T(8,128)(2,1)S(1)}, u32[]{:S(2)}, u32[]{:S(2)}) collective-permute-start(bf16[8,3584]{1,0:T(8,128)(2,1)S(1)} %get-tuple-element.176.refs_4_), channel_id=1, source_target_pairs={{0,64},{1,67},{4,71},{5,68},{8,72},{9,75},{12,79},{13,76},{16,83},... | collective-permute-start | bytes 172040 | tf_op jit(solution)/shard_map/ppermute | solution.py:35
  119.8 4.3 %collective-permute-start.41 = (bf16[8,3584]{1,0:T(8,128)(2,1)S(1)}, bf16[8,3584]{1,0:T(8,128)(2,1)S(1)}, u32[]{:S(2)}, u32[]{:S(2)}) collective-permute-start(bf16[8,3584]{1,0:T(8,128)(2,1)S(1)} %get-tuple-element.183), channel_id=1, source_target_pairs={{0,66},{1,65},{4,69},{5,70},{8,74},{9,73},{12,77},{13,78},{16,81},... | collective-permute-start | bytes 172040 | tf_op jit(solution)/shard_map/ppermute | solution.py:35
  (95 shorter events, 48.4 us)
Async XLA Ops:
  0.6 27.1 %collective-permute-start.9 = (bf16[3584,640]{1,0:T(8,128)(2,1)}, bf16[3584,640]{1,0:T(8,128)(2,1)}, u32[]{:S(2)}, u32[]{:S(2)}) collective-permute-start(bf16[3584,640]{1,0:T(8,128)(2,1)} %h_ref.1), channel_id=1, source_target_pairs={{0,1},{1,0},{2,3},{3,2},{4,5},{5,4},{6,7},{7,6},{8,9},{9,8},{10,11... | collective-permute-start | bytes 13762568 | tf_op jit(solution)/shard_map/ppermute | solution.py:69
  3.0 9.1 %collective-permute-start = (bf16[16,3712]{1,0:T(8,128)(2,1)S(1)}, bf16[16,3712]{1,0:T(8,128)(2,1)S(1)}, u32[]{:S(2)}, u32[]{:S(2)}) collective-permute-start(bf16[16,3712]{1,0:T(8,128)(2,1)S(1)} %shard_map.84.refs_0_), channel_id=1, source_target_pairs={{0,65},{1,66},{4,71},{5,68},{8,73},{9,74},{12,79},{13,76},{16,83},... | collective-permute-start | bytes 356360 | tf_op jit(solution)/shard_map/ppermute | solution.py:35
  6.0 10.6 %collective-permute-start.1 = (bf16[16,3712]{1,0:T(8,128)(2,1)S(1)}, bf16[16,3712]{1,0:T(8,128)(2,1)S(1)}, u32[]{:S(2)}, u32[]{:S(2)}) collective-permute-start(bf16[16,3712]{1,0:T(8,128)(2,1)S(1)} %shard_map.84.refs_0_), channel_id=1, source_target_pairs={{0,5},{1,12},{4,9},{5,0},{8,13},{9,4},{12,1},{13,8},{16,29},{17,20... | collective-permute-start | bytes 356360 | tf_op jit(solution)/shard_map/ppermute | solution.py:35
  8.7 7.8 %collective-permute-start.2 = (bf16[16,3712]{1,0:T(8,128)(2,1)S(1)}, bf16[16,3712]{1,0:T(8,128)(2,1)S(1)}, u32[]{:S(2)}, u32[]{:S(2)}) collective-permute-start(bf16[16,3712]{1,0:T(8,128)(2,1)S(1)} %shard_map.84.refs_0_), channel_id=1, source_target_pairs={{0,13},{1,4},{4,1},{5,8},{8,5},{9,12},{12,9},{13,0},{16,21},{17,28... | collective-permute-start | bytes 356360 | tf_op jit(solution)/shard_map/ppermute | solution.py:35
  8.7 10.2 %collective-permute-start.3 = (bf16[16,3712]{1,0:T(8,128)(2,1)S(1)}, bf16[16,3712]{1,0:T(8,128)(2,1)S(1)}, u32[]{:S(2)}, u32[]{:S(2)}) collective-permute-start(bf16[16,3712]{1,0:T(8,128)(2,1)S(1)} %shard_map.84.refs_0_), channel_id=1, source_target_pairs={{0,8},{1,9},{4,12},{5,13},{8,0},{9,1},{12,4},{13,5},{16,24},{17,25... | collective-permute-start | bytes 356360 | tf_op jit(solution)/shard_map/ppermute | solution.py:35
  12.1 7.5 %collective-permute-start.4 = (bf16[16,3712]{1,0:T(8,128)(2,1)S(1)}, bf16[16,3712]{1,0:T(8,128)(2,1)S(1)}, u32[]{:S(2)}, u32[]{:S(2)}) collective-permute-start(bf16[16,3712]{1,0:T(8,128)(2,1)S(1)} %collective-permute-done.refs_4_), channel_id=1, source_target_pairs={{0,17},{1,48},{4,53},{5,20},{8,25},{9,56},{12,61},{13,28},{16,33},... | collective-permute-start | bytes 356360 | tf_op jit(solution)/shard_map/ppermute | solution.py:35
  23.3 9.4 %collective-permute-start.7 = (bf16[64,3712]{1,0:T(8,128)(2,1)S(1)}, bf16[64,3712]{1,0:T(8,128)(2,1)S(1)}, u32[]{:S(2)}, u32[]{:S(2)}) collective-permute-start(bf16[64,3712]{1,0:T(8,128)(2,1)S(1)} %get-tuple-element.105.refs_0_), channel_id=1, source_target_pairs={{0,17},{1,48},{4,53},{5,20},{8,25},{9,56},{12,61},{13,28},{16,33},... | collective-permute-start | bytes 1425416 | tf_op jit(solution)/shard_map/ppermute | solution.py:35
  25.9 9.3 %collective-permute-start.8 = (bf16[64,3712]{1,0:T(8,128)(2,1)S(1)}, bf16[64,3712]{1,0:T(8,128)(2,1)S(1)}, u32[]{:S(2)}, u32[]{:S(2)}) collective-permute-start(bf16[64,3712]{1,0:T(8,128)(2,1)S(1)} %get-tuple-element.106.refs_2_), channel_id=1, source_target_pairs={{0,5},{1,12},{4,9},{5,0},{8,13},{9,4},{12,1},{13,8},{16,29},{17,20... | collective-permute-start | bytes 1425416 | tf_op jit(solution)/shard_map/ppermute | solution.py:35
  35.3 13.3 %collective-permute-start.10 = (bf16[128,3712]{1,0:T(8,128)(2,1)S(1)}, bf16[128,3712]{1,0:T(8,128)(2,1)S(1)}, u32[]{:S(2)}, u32[]{:S(2)}) collective-permute-start(bf16[128,3712]{1,0:T(8,128)(2,1)S(1)} %get-tuple-element.108.a_ref), channel_id=1, source_target_pairs={{0,49},{1,16},{4,21},{5,52},{8,57},{9,24},{12,29},{13,60},{16,1},{... | collective-permute-start | bytes 2850824 | tf_op jit(solution)/shard_map/ppermute | solution.py:35
  35.4 13.2 %collective-permute-start.11 = (bf16[128,3712]{1,0:T(8,128)(2,1)S(1)}, bf16[128,3712]{1,0:T(8,128)(2,1)S(1)}, u32[]{:S(2)}, u32[]{:S(2)}) collective-permute-start(bf16[128,3712]{1,0:T(8,128)(2,1)S(1)} %get-tuple-element.109.b_ref), channel_id=1, source_target_pairs={{0,13},{1,4},{4,1},{5,8},{8,5},{9,12},{12,9},{13,0},{16,21},{17,28... | collective-permute-start | bytes 2850824 | tf_op jit(solution)/shard_map/ppermute | solution.py:35
  36.2 23.2 %collective-permute-start.13 = (bf16[128,3712]{1,0:T(8,128)(2,1)S(1)}, bf16[128,3712]{1,0:T(8,128)(2,1)S(1)}, u32[]{:S(2)}, u32[]{:S(2)}) collective-permute-start(bf16[128,3712]{1,0:T(8,128)(2,1)S(1)} %get-tuple-element.108.a_ref), channel_id=1, source_target_pairs={{0,1},{1,0},{2,3},{3,2},{4,5},{5,4},{6,7},{7,6},{8,9},{9,8},{10,11... | collective-permute-start | bytes 2850824 | tf_op jit(solution)/shard_map/ppermute | solution.py:69
  36.2 23.3 %collective-permute-start.14 = (bf16[128,3712]{1,0:T(8,128)(2,1)S(1)}, bf16[128,3712]{1,0:T(8,128)(2,1)S(1)}, u32[]{:S(2)}, u32[]{:S(2)}) collective-permute-start(bf16[128,3712]{1,0:T(8,128)(2,1)S(1)} %get-tuple-element.109.b_ref), channel_id=1, source_target_pairs={{0,1},{1,0},{2,3},{3,2},{4,5},{5,4},{6,7},{7,6},{8,9},{9,8},{10,11... | collective-permute-start | bytes 2850824 | tf_op jit(solution)/shard_map/ppermute | solution.py:69
  59.5 11.2 %collective-permute-start.24 = (bf16[128,3712]{1,0:T(8,128)(2,1)S(1)}, bf16[128,3712]{1,0:T(8,128)(2,1)S(1)}, u32[]{:S(2)}, u32[]{:S(2)}) collective-permute-start(bf16[128,3712]{1,0:T(8,128)(2,1)S(1)} %collective-permute-done.10.a_ref), channel_id=1, source_target_pairs={{0,1},{1,0},{2,3},{3,2},{4,5},{5,4},{6,7},{7,6},{8,9},{9,8},{10,11... | collective-permute-start | bytes 2850824 | tf_op jit(solution)/shard_map/ppermute | solution.py:69
  60.0 10.6 %collective-permute-start.25 = (bf16[128,3712]{1,0:T(8,128)(2,1)S(1)}, bf16[128,3712]{1,0:T(8,128)(2,1)S(1)}, u32[]{:S(2)}, u32[]{:S(2)}) collective-permute-start(bf16[128,3712]{1,0:T(8,128)(2,1)S(1)} %collective-permute-done.11.b_ref), channel_id=1, source_target_pairs={{0,1},{1,0},{2,3},{3,2},{4,5},{5,4},{6,7},{7,6},{8,9},{9,8},{10,11... | collective-permute-start | bytes 2850824 | tf_op jit(solution)/shard_map/ppermute | solution.py:69
  76.9 15.0 %collective-permute-start.26 = (bf16[128,3584]{1,0:T(8,128)(2,1)S(1)}, bf16[128,3584]{1,0:T(8,128)(2,1)S(1)}, u32[]{:S(2)}, u32[]{:S(2)}) collective-permute-start(bf16[128,3584]{1,0:T(8,128)(2,1)S(1)} %get-tuple-element.142), channel_id=1, source_target_pairs={{0,49},{1,16},{4,21},{5,52},{8,57},{9,24},{12,29},{13,60},{16,1},{... | collective-permute-start | bytes 2752520 | tf_op jit(solution)/shard_map/ppermute | solution.py:35
  79.8 13.1 %collective-permute-start.27 = (bf16[128,3584]{1,0:T(8,128)(2,1)S(1)}, bf16[128,3584]{1,0:T(8,128)(2,1)S(1)}, u32[]{:S(2)}, u32[]{:S(2)}) collective-permute-start(bf16[128,3584]{1,0:T(8,128)(2,1)S(1)} %get-tuple-element.143), channel_id=1, source_target_pairs={{0,13},{1,4},{4,1},{5,8},{8,5},{9,12},{12,9},{13,0},{16,21},{17,28... | collective-permute-start | bytes 2752520 | tf_op jit(solution)/shard_map/ppermute | solution.py:35
  85.1 6.8 %collective-permute-start.30 = (f32[8,128]{1,0:T(8,128)S(1)}, f32[8,128]{1,0:T(8,128)S(1)}, u32[]{:S(2)}, u32[]{:S(2)}) collective-permute-start(f32[8,128]{1,0:T(8,128)S(1)} %get-tuple-element.179), channel_id=1, source_target_pairs={{0,1},{1,0},{2,3},{3,2},{4,5},{5,4},{6,7},{7,6},{8,9},{9,8},{10,11... | collective-permute-start | bytes 12296 | tf_op jit(solution)/shard_map/ppermute | solution.py:69
  93.3 9.2 %collective-permute-start.31 = (bf16[64,3584]{1,0:T(8,128)(2,1)S(1)}, bf16[64,3584]{1,0:T(8,128)(2,1)S(1)}, u32[]{:S(2)}, u32[]{:S(2)}) collective-permute-start(bf16[64,3584]{1,0:T(8,128)(2,1)S(1)} %get-tuple-element.162), channel_id=1, source_target_pairs={{0,17},{1,48},{4,53},{5,20},{8,25},{9,56},{12,61},{13,28},{16,33},... | collective-permute-start | bytes 1376264 | tf_op jit(solution)/shard_map/ppermute | solution.py:35
  94.3 9.1 %collective-permute-start.32 = (bf16[64,3584]{1,0:T(8,128)(2,1)S(1)}, bf16[64,3584]{1,0:T(8,128)(2,1)S(1)}, u32[]{:S(2)}, u32[]{:S(2)}) collective-permute-start(bf16[64,3584]{1,0:T(8,128)(2,1)S(1)} %get-tuple-element.163), channel_id=1, source_target_pairs={{0,5},{1,12},{4,9},{5,0},{8,13},{9,4},{12,1},{13,8},{16,29},{17,20... | collective-permute-start | bytes 1376264 | tf_op jit(solution)/shard_map/ppermute | solution.py:35
  104.2 6.9 %collective-permute-start.36 = (bf16[16,3584]{1,0:T(8,128)(2,1)S(1)}, bf16[16,3584]{1,0:T(8,128)(2,1)S(1)}, u32[]{:S(2)}, u32[]{:S(2)}) collective-permute-start(bf16[16,3584]{1,0:T(8,128)(2,1)S(1)} %get-tuple-element.173), channel_id=1, source_target_pairs={{0,17},{1,48},{4,53},{5,20},{8,25},{9,56},{12,61},{13,28},{16,33},... | collective-permute-start | bytes 344072 | tf_op jit(solution)/shard_map/ppermute | solution.py:35
  108.4 8.6 %collective-permute-start.33 = (bf16[16,3584]{1,0:T(8,128)(2,1)S(1)}, bf16[16,3584]{1,0:T(8,128)(2,1)S(1)}, u32[]{:S(2)}, u32[]{:S(2)}) collective-permute-start(bf16[16,3584]{1,0:T(8,128)(2,1)S(1)} %get-tuple-element.169), channel_id=1, source_target_pairs={{0,5},{1,12},{4,9},{5,0},{8,13},{9,4},{12,1},{13,8},{16,29},{17,20... | collective-permute-start | bytes 344072 | tf_op jit(solution)/shard_map/ppermute | solution.py:35
  113.7 14.8 %collective-permute-start.40 = (bf16[8,3584]{1,0:T(8,128)(2,1)S(1)}, bf16[8,3584]{1,0:T(8,128)(2,1)S(1)}, u32[]{:S(2)}, u32[]{:S(2)}) collective-permute-start(bf16[8,3584]{1,0:T(8,128)(2,1)S(1)} %get-tuple-element.176.refs_4_), channel_id=1, source_target_pairs={{0,64},{1,67},{4,71},{5,68},{8,72},{9,75},{12,79},{13,76},{16,83},... | collective-permute-start | bytes 172040 | tf_op jit(solution)/shard_map/ppermute | solution.py:35
  117.8 10.7 %collective-permute-start.42 = (bf16[8,3584]{1,0:T(8,128)(2,1)S(1)}, bf16[8,3584]{1,0:T(8,128)(2,1)S(1)}, u32[]{:S(2)}, u32[]{:S(2)}) collective-permute-start(bf16[8,3584]{1,0:T(8,128)(2,1)S(1)} %get-tuple-element.184), channel_id=1, source_target_pairs={{0,2},{1,3},{4,7},{5,6},{8,10},{9,11},{12,15},{13,14},{16,19},{17,... | collective-permute-start | bytes 172040 | tf_op jit(solution)/shard_map/ppermute | solution.py:35
  119.8 8.7 %collective-permute-start.41 = (bf16[8,3584]{1,0:T(8,128)(2,1)S(1)}, bf16[8,3584]{1,0:T(8,128)(2,1)S(1)}, u32[]{:S(2)}, u32[]{:S(2)}) collective-permute-start(bf16[8,3584]{1,0:T(8,128)(2,1)S(1)} %get-tuple-element.183), channel_id=1, source_target_pairs={{0,66},{1,65},{4,69},{5,70},{8,74},{9,73},{12,77},{13,78},{16,81},... | collective-permute-start | bytes 172040 | tf_op jit(solution)/shard_map/ppermute | solution.py:35
  (20 other events, 93.7 us)

commit v2 on v1

--- a/solution.py
+++ b/solution.py
@@ -521,14 +521,15 @@
         other, teacher_send, spot, places, own_group
     )
     teacher_in = swap_core(teacher_send)
-    own, across = [block], [other]
-    for step in range(3):
-        own.append(along(block, True, step))
-    for step in range(3):
-        across.append(along(other, False, step))
+    own_in = along(block, True, 0)
+    across_in = along(other, False, 0)
+    (own,) = joined((block, own_in))
+    own_in = along(own, True, 1)
+    (across,) = joined((other, across_in))
+    across_in = along(across, False, 1)
     teacher = jnp.dot(one_hot(token, tokens, bf16), teacher_logits)
-    *pieces, teacher = together(*own, *across, teacher)
-    near_a, near_b = joined(pieces[:4], pieces[4:], parity=spot)
+    own_in, across_in, teacher = together(own_in, across_in, teacher)
+    near_a, near_b = joined((own, own_in), (across, across_in), parity=spot)
 
     far_a, far_b = swap(near_a, "z", 0), swap(near_b, "x", 0)
     heads, mark = side_by_side(student_head, head_in)
@@ -573,21 +574,22 @@
     keep_a, send_a, keep_b, send_b = added(((near_sum_a, a_in), (near_sum_b, b_in)), 2)
     a_in, b_in = swap(send_a, "z", 0), swap(send_b, "x", 0)
     head_grad = head_gradient(states, all_d, range(4, width // 512), head_grad)
-    a_in, b_in, head_grad = together(a_in, b_in, head_grad)
-    *own, across, to_1, to_2, to_3 = added(((keep_a, a_in), (keep_b, b_in)), 4, spot)
-    across_in = []
-    for step, part in enumerate((to_1, to_2, to_3)):
-        across_in.append(along(part, False, step))
-    own_in = []
-    for step in range(3):
-        own_in.append(along(own[step + 1], True, step))
-    send = added_by_place((across, *across_in), spot, (0, 1))
-    arrived = [to_owner(part, step) for step, part in enumerate(send)]
-    keep, last = added_by_place((own[0], *own_in), spot, (None, 2), after=(send[0],))
-    keep, sums, other_sums = together(keep, sums, other_sums)
-    parts = [to_owner(keep), *arrived, to_owner(last, 2)]
     loss = (sums[0, 0] + other_sums[0, 0]) / (sums[1, 0] + other_sums[1, 0])
     sampled_ratio = jnp.where(own_group, sums[2, :8], other_sums[2, :8])
+    a_in, b_in, head_grad, loss, sampled_ratio = together(
+        a_in, b_in, head_grad, loss, sampled_ratio
+    )
+    own, own_send, across, across_send = added(((keep_a, a_in), (keep_b, b_in)), 2, spot)
+    across_in = along(across_send, False, 1)
+    own_in = along(own_send, True, 1)
+    across, across_send = added(((across, across_in),), 2)
+    across_in = along(across_send, False, 0)
+    own, own_send = added(((own, own_in),), 2)
+    own_in = along(own_send, True, 0)
+    send = added_by_place((across, across_in), spot, (0, 1))
+    arrived = [to_owner(part, step) for step, part in enumerate(send)]
+    keep, last = added_by_place((own, own_in), spot, (None, 2), after=(send[0],))
+    parts = [to_owner(keep), *arrived, to_owner(last, 2)]
     hidden_grad = sum(p.astype(f32) for p in parts).astype(bf16)
     return (loss, sampled_ratio, hidden_grad, head_grad)
 

time: 131 us -> 126 us (0.962)
  starting transfers between devices: 60 us -> 46.8 us
  waiting for transfers between devices: 27.8 us -> 35.4 us
    ppermute x34 -> x30, starting transfers between devices: 54.8 us -> 41.2 us  [moved(): return lax.ppermute(value, TOK_VOC, pairs)]
    ppermute x34 -> x30, waiting for transfers between devices: 25.9 us -> 33.7 us  [moved(): return lax.ppermute(value, TOK_VOC, pairs)]
    pallas_call x21 -> x25, Pallas kernels: 33 us -> 33.1 us  [call(): pl.pallas_call(kernel, out_shape=shapes, in_specs=in_specs, out_specs=out...]
  transfers between devices with their start and end apart: 43 -> 39, of which waited for: 22 -> 19; matrix products, arithmetic and copies ran while one was open for 3% -> 4% of each run, Pallas kernels for 22% -> 22%
where the time goes in v2:
time: 126 us; the launch traced here: 125 us
  starting transfers between devices  46.8 us (37%)
  waiting for transfers between devices  35.4 us (28%)
  Pallas kernels  33.1 us (26%)
  between operations  4.72 us (4%)
  matrix products  2.14 us (2%)
  other arithmetic  2.11 us (2%)
    ppermute x30, starting transfers between devices, moved(): return lax.ppermute(value, TOK_VOC, pairs)  41.2 us
    ppermute x30, waiting for transfers between devices, moved(): return lax.ppermute(value, TOK_VOC, pairs)  33.7 us
    pallas_call x25, Pallas kernels, call(): pl.pallas_call(kernel, out_shape=shapes, in_specs=in_specs, out_specs=out...  33.1 us
    ppermute x9, starting transfers between devices, swap_core(): return lax.ppermute(value, CORE, [(0, 1), (1, 0)])  5.58 us
  transfers between devices with their start and end apart: 39, of which 19 were waited for; matrix products, arithmetic and copies ran while one was open for 4% of the time, Pallas kernels for 22%

profile of v2, /device:TPU:1, one launch (start us, length us, event | category | flops | bytes accessed | tf_op | source)
XLA Modules:
  0.0 125.4 jit_solution(14515905375312492504)
XLA Ops:
  3.0 2.9 %collective-permute-start = (bf16[16,3712]{1,0:T(8,128)(2,1)S(1)}, bf16[16,3712]{1,0:T(8,128)(2,1)S(1)}, u32[]{:S(2)}, u32[]{:S(2)}) collective-permute-start(bf16[16,3712]{1,0:T(8,128)(2,1)S(1)} %shard_map.84.refs_0_), channel_id=1, source_target_pairs={{0,65},{1,66},{4,71},{5,68},{8,73},{9,74},{12,79},{13,76},{16,83},... | collective-permute-start | bytes 356360 | tf_op jit(solution)/shard_map/ppermute | solution.py:35
  6.0 2.8 %collective-permute-start.1 = (bf16[16,3712]{1,0:T(8,128)(2,1)S(1)}, bf16[16,3712]{1,0:T(8,128)(2,1)S(1)}, u32[]{:S(2)}, u32[]{:S(2)}) collective-permute-start(bf16[16,3712]{1,0:T(8,128)(2,1)S(1)} %shard_map.84.refs_0_), channel_id=1, source_target_pairs={{0,5},{1,12},{4,9},{5,0},{8,13},{9,4},{12,1},{13,8},{16,29},{17,20... | collective-permute-start | bytes 356360 | tf_op jit(solution)/shard_map/ppermute | solution.py:35
  10.7 3.8 %collective-permute-start.3 = (bf16[16,3712]{1,0:T(8,128)(2,1)S(1)}, bf16[16,3712]{1,0:T(8,128)(2,1)S(1)}, u32[]{:S(2)}, u32[]{:S(2)}) collective-permute-start(bf16[16,3712]{1,0:T(8,128)(2,1)S(1)} %collective-permute-done.refs_0_), channel_id=1, source_target_pairs={{0,17},{1,48},{4,53},{5,20},{8,25},{9,56},{12,61},{13,28},{16,33},... | collective-permute-start | bytes 356360 | tf_op jit(solution)/shard_map/ppermute | solution.py:35
  14.9 2.2 %collective-permute-done.3.refs_1_ = bf16[16,3712]{1,0:T(8,128)(2,1)S(1)} collective-permute-done((bf16[16,3712]{1,0:T(8,128)(2,1)S(1)}, bf16[16,3712]{1,0:T(8,128)(2,1)S(1)}, u32[]{:S(2)}, u32[]{:S(2)}) %collective-permute-start.3) | collective-permute-done | bytes 118816 | tf_op jit(solution)/shard_map/ppermute | solution.py:35
  18.3 2.0 %collective-permute-done.2.refs_1_ = bf16[32,3712]{1,0:T(8,128)(2,1)S(1)} collective-permute-done((bf16[32,3712]{1,0:T(8,128)(2,1)S(1)}, bf16[32,3712]{1,0:T(8,128)(2,1)S(1)}, u32[]{:S(2)}, u32[]{:S(2)}) %collective-permute-start.2) | collective-permute-done | bytes 237600 | tf_op jit(solution)/shard_map/ppermute | solution.py:35
  20.3 2.5 %collective-permute-done.4.refs_3_ = bf16[32,3712]{1,0:T(8,128)(2,1)S(1)} collective-permute-done((bf16[32,3712]{1,0:T(8,128)(2,1)S(1)}, bf16[32,3712]{1,0:T(8,128)(2,1)S(1)}, u32[]{:S(2)}, u32[]{:S(2)}) %collective-permute-start.4) | collective-permute-done | bytes 237600 | tf_op jit(solution)/shard_map/ppermute | solution.py:35
  23.4 3.0 %collective-permute-start.5 = (bf16[64,3712]{1,0:T(8,128)(2,1)S(1)}, bf16[64,3712]{1,0:T(8,128)(2,1)S(1)}, u32[]{:S(2)}, u32[]{:S(2)}) collective-permute-start(bf16[64,3712]{1,0:T(8,128)(2,1)S(1)} %get-tuple-element.92.refs_0_), channel_id=1, source_target_pairs={{0,17},{1,48},{4,53},{5,20},{8,25},{9,56},{12,61},{13,28},{16,33},... | collective-permute-start | bytes 1425416 | tf_op jit(solution)/shard_map/ppermute | solution.py:35
  27.3 3.7 %shard_map.88 = (bf16[3584,1280]{1,0:T(8,128)(2,1)S(1)}, f32[8,128]{1,0:T(8,128)S(1)}) custom-call(bf16[3584,640]{1,0:T(8,128)(2,1)} %h_ref.1, bf16[3584,640]{1,0:T(8,128)(2,1)} %collective-permute-done.7.g_ref), custom_call_target="tpu_custom_call" | custom-call | flops 4000000000 | bytes 1000000 | tf_op jit(solution)/shard_map/pallas_call | solution.py:121
  32.7 3.2 %collective-permute-done.6.refs_3_ = bf16[64,3712]{1,0:T(8,128)(2,1)S(1)} collective-permute-done((bf16[64,3712]{1,0:T(8,128)(2,1)S(1)}, bf16[64,3712]{1,0:T(8,128)(2,1)S(1)}, u32[]{:S(2)}, u32[]{:S(2)}) %collective-permute-start.6) | collective-permute-done | bytes 475168 | tf_op jit(solution)/shard_map/ppermute | solution.py:35
  38.5 3.8 %shard_map.90 = (f32[256,1280]{1,0:T(8,128)S(1)}, f32[8,512]{1,0:T(8,128)S(1)}) custom-call(s32[4]{0:T(128)S(1)} %pad_add_fusion.refs_4_.spot_ref, bf16[128,3712]{1,0:T(8,128)(2,1)S(1)} %get-tuple-element.95.a_ref, bf16[128,3712]{1,0:T(8,128)(2,1)S(1)} %get-tuple-element.96.b_ref, bf16[3584,1280]{1,0:T(8,128)(2,1)S(1)} %get-tuple-element.97.h_ref, ...), custom_call_target="tpu_custom_call" | custom-call | flops 2348810240 | bytes 1000000 | tf_op jit(solution)/shard_map/pallas_call | solution.py:121
  42.3 7.1 %collective-permute-done.8.a_ref = bf16[128,3712]{1,0:T(8,128)(2,1)S(1)} collective-permute-done((bf16[128,3712]{1,0:T(8,128)(2,1)S(1)}, bf16[128,3712]{1,0:T(8,128)(2,1)S(1)}, u32[]{:S(2)}, u32[]{:S(2)}) %collective-permute-start.8) | collective-permute-done | bytes 950304 | tf_op jit(solution)/shard_map/ppermute | solution.py:35
  49.5 3.8 %shard_map.92 = (f32[256,1280]{1,0:T(8,128)S(1)}, f32[8,512]{1,0:T(8,128)S(1)}) custom-call(s32[4]{0:T(128)S(1)} %pad_add_fusion.refs_4_.spot_ref, bf16[128,3712]{1,0:T(8,128)(2,1)S(1)} %collective-permute-done.8.a_ref, bf16[128,3712]{1,0:T(8,128)(2,1)S(1)} %collective-permute-done.9.b_ref, bf16[3584,1280]{1,0:T(8,128)(2,1)S(1)} %get-tuple-element.97.h_ref, ...), custom_call_target="tpu_custom_call" | custom-call | flops 2348810240 | bytes 1000000 | tf_op jit(solution)/shard_map/pallas_call | solution.py:121
  54.0 3.5 %collective-permute-start.15 = (f32[8,512]{1,0:T(8,128)S(1)}, f32[8,512]{1,0:T(8,128)S(1)}, u32[]{:S(2)}, u32[]{:S(2)}) collective-permute-start(f32[8,512]{1,0:T(8,128)S(1)} %get-tuple-element.108.refs_0_), channel_id=1, source_target_pairs={{0,8},{1,9},{4,12},{5,13},{8,0},{9,1},{12,4},{13,5},{16,24},{17,25... | collective-permute-start | bytes 49160 | tf_op jit(solution)/shard_map/ppermute | solution.py:35
  60.1 1.9 %collective-permute-start.17 = (f32[8,512]{1,0:T(8,128)S(1)}, f32[8,512]{1,0:T(8,128)S(1)}, u32[]{:S(2)}, u32[]{:S(2)}) collective-permute-start(f32[8,512]{1,0:T(8,128)S(1)} %shard_map.94.refs_0_), channel_id=1, source_target_pairs={{0,49},{1,16},{4,21},{5,52},{8,57},{9,24},{12,29},{13,60},{16,1},{... | collective-permute-start | bytes 49160 | tf_op jit(solution)/shard_map/ppermute | solution.py:35
  66.1 2.8 %collective-permute-start.19 = (f32[8,512]{1,0:T(8,128)S(1)}, f32[8,512]{1,0:T(8,128)S(1)}, u32[]{:S(2)}, u32[]{:S(2)}) collective-permute-start(f32[8,512]{1,0:T(8,128)S(1)} %shard_map.96.refs_0_), channel_id=1, source_target_pairs={{0,65},{1,66},{4,71},{5,68},{8,73},{9,74},{12,79},{13,76},{16,83},... | collective-permute-start | bytes 49160 | tf_op jit(solution)/shard_map/ppermute | solution.py:35
  73.8 3.1 %shard_map.99 = (bf16[128,3584]{1,0:T(8,128)(2,1)S(1)}, bf16[128,3584]{1,0:T(8,128)(2,1)S(1)}, bf16[256,640]{1,0:T(8,128)(2,1)S(1)}, bf16[256,640]{1,0:T(8,128)(2,1)S(1)}) custom-call(f32[256,1280]{1,0:T(8,128)S(1)} %get-tuple-element.106.s_ref, f32[8,512]{1,0:T(8,128)S(1)} %get-tuple-element.132.c_ref, bf16[3584,1280]{1,0:T(8,128)(2,1)S(1)} %get-tuple-element.97.h_ref, ...), custom_call_target="tpu_custom_call" | custom-call | flops 2348810240 | bytes 1000000 | tf_op jit(solution)/shard_map/pallas_call | solution.py:121
  79.4 3.1 %shard_map.100 = (bf16[128,3584]{1,0:T(8,128)(2,1)S(1)}, bf16[128,3584]{1,0:T(8,128)(2,1)S(1)}, bf16[256,640]{1,0:T(8,128)(2,1)S(1)}, bf16[256,640]{1,0:T(8,128)(2,1)S(1)}) custom-call(f32[256,1280]{1,0:T(8,128)S(1)} %get-tuple-element.131.s_ref, f32[8,512]{1,0:T(8,128)S(1)} %get-tuple-element.132.c_ref, bf16[3584,1280]{1,0:T(8,128)(2,1)S(1)} %get-tuple-element.97.h_ref, ...), custom_call_target="tpu_custom_call" | custom-call | flops 2348810240 | bytes 1000000 | tf_op jit(solution)/shard_map/pallas_call | solution.py:121
  82.5 2.3 %collective-permute-start.26 = (bf16[256,640]{1,0:T(8,128)(2,1)S(1)}, bf16[256,640]{1,0:T(8,128)(2,1)S(1)}, u32[]{:S(2)}, u32[]{:S(2)}) collective-permute-start(bf16[256,640]{1,0:T(8,128)(2,1)S(1)} %get-tuple-element.141), channel_id=1, source_target_pairs={{0,1},{1,0},{2,3},{3,2},{4,5},{5,4},{6,7},{7,6},{8,9},{9,8},{10,11... | collective-permute-start | bytes 983048 | tf_op jit(solution)/shard_map/ppermute | solution.py:69
  86.6 5.2 %shard_map.101.refs_8_ = bf16[3584,640]{1,0:T(8,128)(2,1)} custom-call(bf16[3584,256]{1,0:T(8,128)(2,1)S(1)} %shard_map.91.refs_0_, bf16[3584,256]{1,0:T(8,128)(2,1)S(1)} %shard_map.93.refs_1_, bf16[3584,256]{1,0:T(8,128)(2,1)S(1)} %shard_map.95.refs_2_, bf16[3584,256]{1,0:T(8,128)(2,1)S(1)} %shard_map.97.refs_3_, ...), custom_call_target="tpu_custom_call" | custom-call | flops 2684354560 | bytes 1000000 | tf_op jit(solution)/shard_map/pallas_call | solution.py:121
  92.2 2.0 %collective-permute-start.29 = (bf16[64,3584]{1,0:T(8,128)(2,1)S(1)}, bf16[64,3584]{1,0:T(8,128)(2,1)S(1)}, u32[]{:S(2)}, u32[]{:S(2)}) collective-permute-start(bf16[64,3584]{1,0:T(8,128)(2,1)S(1)} %get-tuple-element.148), channel_id=1, source_target_pairs={{0,17},{1,48},{4,53},{5,20},{8,25},{9,56},{12,61},{13,28},{16,33},... | collective-permute-start | bytes 1376264 | tf_op jit(solution)/shard_map/ppermute | solution.py:35
  99.1 3.6 %shard_map.103 = bf16[3584,640]{1,0:T(8,128)(2,1)} custom-call(bf16[3584,256]{1,0:T(8,128)(2,1)S(1)} %shard_map.91.refs_0_, bf16[3584,256]{1,0:T(8,128)(2,1)S(1)} %shard_map.93.refs_1_, bf16[3584,256]{1,0:T(8,128)(2,1)S(1)} %shard_map.95.refs_2_, bf16[3584,256]{1,0:T(8,128)(2,1)S(1)} %shard_map.97.refs_3_, ...), custom_call_target="tpu_custom_call", output_to_operand_aliasing={{}: (8, {})} | custom-call | flops 2013265920 | bytes 1000000 | tf_op jit(solution)/shard_map/pallas_call | solution.py:121
  105.3 4.6 %collective-permute-done.33.refs_1_ = bf16[32,3584]{1,0:T(8,128)(2,1)S(1)} collective-permute-done((bf16[32,3584]{1,0:T(8,128)(2,1)S(1)}, bf16[32,3584]{1,0:T(8,128)(2,1)S(1)}, u32[]{:S(2)}, u32[]{:S(2)}) %collective-permute-start.33) | collective-permute-done | bytes 229408 | tf_op jit(solution)/shard_map/ppermute | solution.py:35
  112.2 3.3 %collective-permute-done.34.refs_1_ = bf16[16,3584]{1,0:T(8,128)(2,1)S(1)} collective-permute-done((bf16[16,3584]{1,0:T(8,128)(2,1)S(1)}, bf16[16,3584]{1,0:T(8,128)(2,1)S(1)}, u32[]{:S(2)}, u32[]{:S(2)}) %collective-permute-start.34) | collective-permute-done | bytes 114720 | tf_op jit(solution)/shard_map/ppermute | solution.py:35
  117.9 1.8 %collective-permute-start.38 = (bf16[8,3584]{1,0:T(8,128)(2,1)S(1)}, bf16[8,3584]{1,0:T(8,128)(2,1)S(1)}, u32[]{:S(2)}, u32[]{:S(2)}) collective-permute-start(bf16[8,3584]{1,0:T(8,128)(2,1)S(1)} %get-tuple-element.170), channel_id=1, source_target_pairs={{0,2},{1,3},{4,7},{5,6},{8,10},{9,11},{12,15},{13,14},{16,19},{17,... | collective-permute-start | bytes 172040 | tf_op jit(solution)/shard_map/ppermute | solution.py:35
  (92 shorter events, 42.8 us)
Async XLA Ops:
  0.6 26.7 %collective-permute-start.7 = (bf16[3584,640]{1,0:T(8,128)(2,1)}, bf16[3584,640]{1,0:T(8,128)(2,1)}, u32[]{:S(2)}, u32[]{:S(2)}) collective-permute-start(bf16[3584,640]{1,0:T(8,128)(2,1)} %h_ref.1), channel_id=1, source_target_pairs={{0,1},{1,0},{2,3},{3,2},{4,5},{5,4},{6,7},{7,6},{8,9},{9,8},{10,11... | collective-permute-start | bytes 13762568 | tf_op jit(solution)/shard_map/ppermute | solution.py:69
  3.0 7.7 %collective-permute-start = (bf16[16,3712]{1,0:T(8,128)(2,1)S(1)}, bf16[16,3712]{1,0:T(8,128)(2,1)S(1)}, u32[]{:S(2)}, u32[]{:S(2)}) collective-permute-start(bf16[16,3712]{1,0:T(8,128)(2,1)S(1)} %shard_map.84.refs_0_), channel_id=1, source_target_pairs={{0,65},{1,66},{4,71},{5,68},{8,73},{9,74},{12,79},{13,76},{16,83},... | collective-permute-start | bytes 356360 | tf_op jit(solution)/shard_map/ppermute | solution.py:35
  6.0 8.7 %collective-permute-start.1 = (bf16[16,3712]{1,0:T(8,128)(2,1)S(1)}, bf16[16,3712]{1,0:T(8,128)(2,1)S(1)}, u32[]{:S(2)}, u32[]{:S(2)}) collective-permute-start(bf16[16,3712]{1,0:T(8,128)(2,1)S(1)} %shard_map.84.refs_0_), channel_id=1, source_target_pairs={{0,5},{1,12},{4,9},{5,0},{8,13},{9,4},{12,1},{13,8},{16,29},{17,20... | collective-permute-start | bytes 356360 | tf_op jit(solution)/shard_map/ppermute | solution.py:35
  10.7 6.4 %collective-permute-start.3 = (bf16[16,3712]{1,0:T(8,128)(2,1)S(1)}, bf16[16,3712]{1,0:T(8,128)(2,1)S(1)}, u32[]{:S(2)}, u32[]{:S(2)}) collective-permute-start(bf16[16,3712]{1,0:T(8,128)(2,1)S(1)} %collective-permute-done.refs_0_), channel_id=1, source_target_pairs={{0,17},{1,48},{4,53},{5,20},{8,25},{9,56},{12,61},{13,28},{16,33},... | collective-permute-start | bytes 356360 | tf_op jit(solution)/shard_map/ppermute | solution.py:35
  14.6 5.6 %collective-permute-start.2 = (bf16[32,3712]{1,0:T(8,128)(2,1)S(1)}, bf16[32,3712]{1,0:T(8,128)(2,1)S(1)}, u32[]{:S(2)}, u32[]{:S(2)}) collective-permute-start(bf16[32,3712]{1,0:T(8,128)(2,1)S(1)} %shard_map.85.refs_0_), channel_id=1, source_target_pairs={{0,13},{1,4},{4,1},{5,8},{8,5},{9,12},{12,9},{13,0},{16,21},{17,28... | collective-permute-start | bytes 712712 | tf_op jit(solution)/shard_map/ppermute | solution.py:35
  17.1 5.6 %collective-permute-start.4 = (bf16[32,3712]{1,0:T(8,128)(2,1)S(1)}, bf16[32,3712]{1,0:T(8,128)(2,1)S(1)}, u32[]{:S(2)}, u32[]{:S(2)}) collective-permute-start(bf16[32,3712]{1,0:T(8,128)(2,1)S(1)} %shard_map.86.refs_2_), channel_id=1, source_target_pairs={{0,49},{1,16},{4,21},{5,52},{8,57},{9,24},{12,29},{13,60},{16,1},{... | collective-permute-start | bytes 712712 | tf_op jit(solution)/shard_map/ppermute | solution.py:35
  23.4 9.4 %collective-permute-start.5 = (bf16[64,3712]{1,0:T(8,128)(2,1)S(1)}, bf16[64,3712]{1,0:T(8,128)(2,1)S(1)}, u32[]{:S(2)}, u32[]{:S(2)}) collective-permute-start(bf16[64,3712]{1,0:T(8,128)(2,1)S(1)} %get-tuple-element.92.refs_0_), channel_id=1, source_target_pairs={{0,17},{1,48},{4,53},{5,20},{8,25},{9,56},{12,61},{13,28},{16,33},... | collective-permute-start | bytes 1425416 | tf_op jit(solution)/shard_map/ppermute | solution.py:35
  26.4 9.6 %collective-permute-start.6 = (bf16[64,3712]{1,0:T(8,128)(2,1)S(1)}, bf16[64,3712]{1,0:T(8,128)(2,1)S(1)}, u32[]{:S(2)}, u32[]{:S(2)}) collective-permute-start(bf16[64,3712]{1,0:T(8,128)(2,1)S(1)} %get-tuple-element.93.refs_2_), channel_id=1, source_target_pairs={{0,5},{1,12},{4,9},{5,0},{8,13},{9,4},{12,1},{13,8},{16,29},{17,20... | collective-permute-start | bytes 1425416 | tf_op jit(solution)/shard_map/ppermute | solution.py:35
  36.1 13.3 %collective-permute-start.8 = (bf16[128,3712]{1,0:T(8,128)(2,1)S(1)}, bf16[128,3712]{1,0:T(8,128)(2,1)S(1)}, u32[]{:S(2)}, u32[]{:S(2)}) collective-permute-start(bf16[128,3712]{1,0:T(8,128)(2,1)S(1)} %get-tuple-element.95.a_ref), channel_id=1, source_target_pairs={{0,49},{1,16},{4,21},{5,52},{8,57},{9,24},{12,29},{13,60},{16,1},{... | collective-permute-start | bytes 2850824 | tf_op jit(solution)/shard_map/ppermute | solution.py:35
  36.2 13.2 %collective-permute-start.9 = (bf16[128,3712]{1,0:T(8,128)(2,1)S(1)}, bf16[128,3712]{1,0:T(8,128)(2,1)S(1)}, u32[]{:S(2)}, u32[]{:S(2)}) collective-permute-start(bf16[128,3712]{1,0:T(8,128)(2,1)S(1)} %get-tuple-element.96.b_ref), channel_id=1, source_target_pairs={{0,13},{1,4},{4,1},{5,8},{8,5},{9,12},{12,9},{13,0},{16,21},{17,28... | collective-permute-start | bytes 2850824 | tf_op jit(solution)/shard_map/ppermute | solution.py:35
  36.4 22.4 %collective-permute-start.11 = (bf16[128,3712]{1,0:T(8,128)(2,1)S(1)}, bf16[128,3712]{1,0:T(8,128)(2,1)S(1)}, u32[]{:S(2)}, u32[]{:S(2)}) collective-permute-start(bf16[128,3712]{1,0:T(8,128)(2,1)S(1)} %get-tuple-element.95.a_ref), channel_id=1, source_target_pairs={{0,1},{1,0},{2,3},{3,2},{4,5},{5,4},{6,7},{7,6},{8,9},{9,8},{10,11... | collective-permute-start | bytes 2850824 | tf_op jit(solution)/shard_map/ppermute | solution.py:69
  36.9 21.9 %collective-permute-start.12 = (bf16[128,3712]{1,0:T(8,128)(2,1)S(1)}, bf16[128,3712]{1,0:T(8,128)(2,1)S(1)}, u32[]{:S(2)}, u32[]{:S(2)}) collective-permute-start(bf16[128,3712]{1,0:T(8,128)(2,1)S(1)} %get-tuple-element.96.b_ref), channel_id=1, source_target_pairs={{0,1},{1,0},{2,3},{3,2},{4,5},{5,4},{6,7},{7,6},{8,9},{9,8},{10,11... | collective-permute-start | bytes 2850824 | tf_op jit(solution)/shard_map/ppermute | solution.py:69
  58.8 11.9 %collective-permute-start.22 = (bf16[128,3712]{1,0:T(8,128)(2,1)S(1)}, bf16[128,3712]{1,0:T(8,128)(2,1)S(1)}, u32[]{:S(2)}, u32[]{:S(2)}) collective-permute-start(bf16[128,3712]{1,0:T(8,128)(2,1)S(1)} %collective-permute-done.8.a_ref), channel_id=1, source_target_pairs={{0,1},{1,0},{2,3},{3,2},{4,5},{5,4},{6,7},{7,6},{8,9},{9,8},{10,11... | collective-permute-start | bytes 2850824 | tf_op jit(solution)/shard_map/ppermute | solution.py:69
  58.9 11.8 %collective-permute-start.23 = (bf16[128,3712]{1,0:T(8,128)(2,1)S(1)}, bf16[128,3712]{1,0:T(8,128)(2,1)S(1)}, u32[]{:S(2)}, u32[]{:S(2)}) collective-permute-start(bf16[128,3712]{1,0:T(8,128)(2,1)S(1)} %collective-permute-done.9.b_ref), channel_id=1, source_target_pairs={{0,1},{1,0},{2,3},{3,2},{4,5},{5,4},{6,7},{7,6},{8,9},{9,8},{10,11... | collective-permute-start | bytes 2850824 | tf_op jit(solution)/shard_map/ppermute | solution.py:69
  76.8 14.9 %collective-permute-start.24 = (bf16[128,3584]{1,0:T(8,128)(2,1)S(1)}, bf16[128,3584]{1,0:T(8,128)(2,1)S(1)}, u32[]{:S(2)}, u32[]{:S(2)}) collective-permute-start(bf16[128,3584]{1,0:T(8,128)(2,1)S(1)} %get-tuple-element.129), channel_id=1, source_target_pairs={{0,49},{1,16},{4,21},{5,52},{8,57},{9,24},{12,29},{13,60},{16,1},{... | collective-permute-start | bytes 2752520 | tf_op jit(solution)/shard_map/ppermute | solution.py:35
  78.2 13.6 %collective-permute-start.25 = (bf16[128,3584]{1,0:T(8,128)(2,1)S(1)}, bf16[128,3584]{1,0:T(8,128)(2,1)S(1)}, u32[]{:S(2)}, u32[]{:S(2)}) collective-permute-start(bf16[128,3584]{1,0:T(8,128)(2,1)S(1)} %get-tuple-element.130), channel_id=1, source_target_pairs={{0,13},{1,4},{4,1},{5,8},{8,5},{9,12},{12,9},{13,0},{16,21},{17,28... | collective-permute-start | bytes 2752520 | tf_op jit(solution)/shard_map/ppermute | solution.py:35
  84.9 6.8 %collective-permute-start.28 = (f32[8,128]{1,0:T(8,128)S(1)}, f32[8,128]{1,0:T(8,128)S(1)}, u32[]{:S(2)}, u32[]{:S(2)}) collective-permute-start(f32[8,128]{1,0:T(8,128)S(1)} %get-tuple-element.143), channel_id=1, source_target_pairs={{0,1},{1,0},{2,3},{3,2},{4,5},{5,4},{6,7},{7,6},{8,9},{9,8},{10,11... | collective-permute-start | bytes 12296 | tf_op jit(solution)/shard_map/ppermute | solution.py:69
  92.2 11.0 %collective-permute-start.29 = (bf16[64,3584]{1,0:T(8,128)(2,1)S(1)}, bf16[64,3584]{1,0:T(8,128)(2,1)S(1)}, u32[]{:S(2)}, u32[]{:S(2)}) collective-permute-start(bf16[64,3584]{1,0:T(8,128)(2,1)S(1)} %get-tuple-element.148), channel_id=1, source_target_pairs={{0,17},{1,48},{4,53},{5,20},{8,25},{9,56},{12,61},{13,28},{16,33},... | collective-permute-start | bytes 1376264 | tf_op jit(solution)/shard_map/ppermute | solution.py:35
  94.2 9.1 %collective-permute-start.30 = (bf16[64,3584]{1,0:T(8,128)(2,1)S(1)}, bf16[64,3584]{1,0:T(8,128)(2,1)S(1)}, u32[]{:S(2)}, u32[]{:S(2)}) collective-permute-start(bf16[64,3584]{1,0:T(8,128)(2,1)S(1)} %get-tuple-element.149), channel_id=1, source_target_pairs={{0,5},{1,12},{4,9},{5,0},{8,13},{9,4},{12,1},{13,8},{16,29},{17,20... | collective-permute-start | bytes 1376264 | tf_op jit(solution)/shard_map/ppermute | solution.py:35
  104.1 5.8 %collective-permute-start.33 = (bf16[32,3584]{1,0:T(8,128)(2,1)S(1)}, bf16[32,3584]{1,0:T(8,128)(2,1)S(1)}, u32[]{:S(2)}, u32[]{:S(2)}) collective-permute-start(bf16[32,3584]{1,0:T(8,128)(2,1)S(1)} %get-tuple-element.164), channel_id=1, source_target_pairs={{0,49},{1,16},{4,21},{5,52},{8,57},{9,24},{12,29},{13,60},{16,1},{... | collective-permute-start | bytes 688136 | tf_op jit(solution)/shard_map/ppermute | solution.py:35
  104.6 6.2 %collective-permute-start.31 = (bf16[32,3584]{1,0:T(8,128)(2,1)S(1)}, bf16[32,3584]{1,0:T(8,128)(2,1)S(1)}, u32[]{:S(2)}, u32[]{:S(2)}) collective-permute-start(bf16[32,3584]{1,0:T(8,128)(2,1)S(1)} %get-tuple-element.160), channel_id=1, source_target_pairs={{0,13},{1,4},{4,1},{5,8},{8,5},{9,12},{12,9},{13,0},{16,21},{17,28... | collective-permute-start | bytes 688136 | tf_op jit(solution)/shard_map/ppermute | solution.py:35
  110.0 5.5 %collective-permute-start.34 = (bf16[16,3584]{1,0:T(8,128)(2,1)S(1)}, bf16[16,3584]{1,0:T(8,128)(2,1)S(1)}, u32[]{:S(2)}, u32[]{:S(2)}) collective-permute-start(bf16[16,3584]{1,0:T(8,128)(2,1)S(1)} %get-tuple-element.166), channel_id=1, source_target_pairs={{0,17},{1,48},{4,53},{5,20},{8,25},{9,56},{12,61},{13,28},{16,33},... | collective-permute-start | bytes 344072 | tf_op jit(solution)/shard_map/ppermute | solution.py:35
  110.9 6.4 %collective-permute-start.32 = (bf16[16,3584]{1,0:T(8,128)(2,1)S(1)}, bf16[16,3584]{1,0:T(8,128)(2,1)S(1)}, u32[]{:S(2)}, u32[]{:S(2)}) collective-permute-start(bf16[16,3584]{1,0:T(8,128)(2,1)S(1)} %get-tuple-element.162), channel_id=1, source_target_pairs={{0,5},{1,12},{4,9},{5,0},{8,13},{9,4},{12,1},{13,8},{16,29},{17,20... | collective-permute-start | bytes 344072 | tf_op jit(solution)/shard_map/ppermute | solution.py:35
  116.1 7.5 %collective-permute-start.36 = (bf16[8,3584]{1,0:T(8,128)(2,1)S(1)}, bf16[8,3584]{1,0:T(8,128)(2,1)S(1)}, u32[]{:S(2)}, u32[]{:S(2)}) collective-permute-start(bf16[8,3584]{1,0:T(8,128)(2,1)S(1)} %get-tuple-element.167.refs_2_), channel_id=1, source_target_pairs={{0,64},{1,67},{4,71},{5,68},{8,72},{9,75},{12,79},{13,76},{16,83},... | collective-permute-start | bytes 172040 | tf_op jit(solution)/shard_map/ppermute | solution.py:35
  (16 other events, 67.6 us)
